TPU v7x, 256 devices: a whole 4x4x8 slice. The times are simulated.
256 devices in a mesh: rep: 32 (over z_lo, x, core), ep: 8 (over z_hi, y).
Axes of the slice: x: 4, y: 4, z: 8 (z_hi: 2, z_lo: 4; z = z_hi * 4 + z_lo), core: 2. Of those that a mesh axis runs over, the one named last changes fastest.
Arguments:
- tokens: bfloat16 [2, 1024, 4096], P(None, 'ep', 'rep'), may hold values from -6 to 6
- expert_ids: int32 [2, 1024, 2], P(None, 'ep'), may hold values from 0 to 7, all different within a row; in each aligned block of 128 rows (0 to 127, 128 to 255, ..., all dimensions but the last counted through in order) at most 48 rows name the same one
- router_weight: bfloat16 [4096, 8], P('rep'), may hold values from -0.09375 to 0.09375
- w_gate: bfloat16 [8, 4096, 8192], P('ep', None, 'rep'), may hold values from -0.09375 to 0.09375
- w_up: bfloat16 [8, 4096, 8192], P('ep', None, 'rep'), may hold values from -0.09375 to 0.09375
- w_down: bfloat16 [8, 8192, 4096], P('ep', 'rep'), may hold values from -0.0625 to 0.0625
- cotangent: bfloat16 [2, 1024, 4096], P(None, 'ep', 'rep'), may hold values from -6 to 6
Outputs:
- mixed: bfloat16 [2, 1024, 4096], P(None, 'ep', 'rep')
- token_grad: bfloat16 [2, 1024, 4096], P(None, 'ep', 'rep')
- gate_grad: bfloat16 [8, 4096, 8192], P('ep', None, 'rep')
- up_grad: bfloat16 [8, 4096, 8192], P('ep', None, 'rep')
- down_grad: bfloat16 [8, 8192, 4096], P('ep', 'rep')
- router_grad: float32 [4096, 8], P('rep')
Inputs may be any that keep to these rules, and one draw needn't show every extreme that they name: `expert_ids`: each row names 2 different experts. Among the 128 rows of one index of ep in one microbatch no expert is named by more than 48 rows, and in every draw some expert is named by exactly 48 of them.
All inputs are finite; a program needn't handle non-finite values.
Results may differ from a plain program's by a relative error of at most 0.025.
Values may be sent and summed in bfloat16 or wider, within the bound.
A program may use at most 128 MiB of HBM per device.

v0:
```python
import jax
import jax.numpy as jnp
from jax import lax
from jax.sharding import Mesh
from jax.sharding import PartitionSpec as P

TOP = 2
REP = ("rep_0", "rep_1", "rep_2")


def copy_for_each(array, axis):
    devices = lax.axis_size(axis)
    return lax.all_to_all(
        jnp.broadcast_to(array[None], (devices, *array.shape)), axis, 0, 0, tiled=True
    )


def taken_together(array, axis):
    everything = copy_for_each(array, axis)
    return jnp.sum(everything, axis=0)


def split_up(array, dim, devices):
    dims = array.shape
    blocks = array.reshape(*dims[:dim], devices, dims[dim] // devices, *dims[dim + 1 :])
    return jnp.moveaxis(blocks, dim, 0)


def summed_on_arrival(array, axis, dim):
    blocks = split_up(array, dim, lax.axis_size(axis))
    arrived = lax.all_to_all(blocks, axis, split_axis=0, concat_axis=0, tiled=True)
    return arrived.astype(jnp.float32).sum(axis=0)


def sum_by_axis(array, axes, dim):
    far, near = axes
    blocks = split_up(array, dim, lax.axis_size(far))
    nearer = summed_on_arrival(blocks, near, dim + 1)
    arrived = lax.all_to_all(
        nearer.astype(jnp.bfloat16), far, split_axis=0, concat_axis=0, tiled=True
    )
    return arrived.astype(jnp.float32).sum(axis=0)


def contract_first(left, right):
    return lax.dot_general(
        left, right, (((0,), (0,)), ((), ())), preferred_element_type=jnp.float32
    )


def contract_last(left, right):
    return lax.dot_general(
        left, right, (((1,), (1,)), ((), ())), preferred_element_type=jnp.float32
    )


def route(route_ids, experts, capacity, slot_count):
    hits = route_ids[:, :, None] == jnp.arange(experts, dtype=jnp.int32)[None, None, :]
    per_token = jnp.sum(hits.astype(jnp.int32), axis=1)
    before = jnp.cumsum(per_token, axis=0) - per_token
    places = jnp.sum(jnp.where(hits, before[:, None, :], 0), axis=2)
    slots = route_ids * capacity + places
    match = jnp.arange(slot_count, dtype=jnp.int32)[:, None, None] == slots[None, :, :]
    token_count = route_ids.shape[0]
    source_row = jnp.sum(
        jnp.where(match, jnp.arange(token_count, dtype=jnp.int32)[None, :, None], 0), axis=(1, 2)
    )
    filled = jnp.any(match, axis=(1, 2))
    return (hits, slots, match, source_row, filled)


def pack(rows, source_row, filled, scale):
    picked = jnp.take(rows, source_row, axis=0)
    if scale is None:
        return jnp.where(filled[:, None], picked, jnp.zeros_like(picked))
    return (picked.astype(jnp.float32) * scale[:, None]).astype(jnp.bfloat16)


def deliver(rows, source_row, filled, scale):
    moved = lax.all_to_all(
        pack(rows, source_row, filled, scale), "ep", split_axis=0, concat_axis=0, tiled=True
    )
    result = lax.all_gather(moved, REP, axis=1, tiled=True)
    return result


def collect(columns):
    return lax.all_to_all(columns, "ep", split_axis=1, concat_axis=1, tiled=True)


def shards(tokens, expert_ids, router_weight, w_gate, w_up, w_down, cotangent):
    micro_count = tokens.shape[0]
    tok_rows = tokens.shape[1]
    experts = router_weight.shape[1]
    capacity = min(tok_rows, 3 * tok_rows * TOP // (2 * experts))
    slot_count = lax.axis_size("ep") * capacity
    gate_w = w_gate[0]
    up_w = w_up[0]
    down_w = w_down[0]
    gate_acc = jnp.zeros(gate_w.shape, jnp.float32)
    up_acc = jnp.zeros(up_w.shape, jnp.float32)
    down_acc = jnp.zeros(down_w.shape, jnp.float32)
    router_acc = jnp.zeros(router_weight.shape, jnp.float32)
    router_wide = router_weight.astype(jnp.float32)
    all_logits = taken_together(
        jnp.einsum("mtc,ce->mte", tokens, router_weight, preferred_element_type=jnp.float32), REP
    )
    mixed = []
    token_grad = []
    for step in range(micro_count):
        route_ids = expert_ids[step]
        hits, slots, match, source_row, filled = route(route_ids, experts, capacity, slot_count)
        logits = all_logits[step]
        chosen = jnp.sum(jnp.where(hits, logits[:, None, :], 0.0), axis=2)
        spread = chosen[:, 0] - chosen[:, 1]
        first = jax.nn.sigmoid(spread)
        second = jax.nn.sigmoid(-spread)
        gates = jnp.stack([first, second], axis=1)
        slot_gate = jnp.sum(jnp.where(match, gates[None, :, :], 0.0), axis=(1, 2))
        expert_rows = deliver(tokens[step], source_row, filled, None)
        pre_gate = jnp.dot(expert_rows, gate_w, preferred_element_type=jnp.float32)
        pre_up = jnp.dot(expert_rows, up_w, preferred_element_type=jnp.float32)
        gate_sig = jax.nn.sigmoid(pre_gate)
        gate_act = pre_gate * gate_sig
        hidden = (gate_act * pre_up).astype(jnp.bfloat16)
        outputs = sum_by_axis(
            lax.dot_general(
                down_w, hidden, (((0,), (1,)), ((), ())), preferred_element_type=jnp.float32
            ).astype(jnp.bfloat16),
            (("rep_0", "rep_1"), "rep_2"),
            0,
        ).astype(jnp.bfloat16)
        returned = collect(outputs)
        first_out = jnp.take(returned, slots[:, 0], axis=1).astype(jnp.float32)
        second_out = jnp.take(returned, slots[:, 1], axis=1).astype(jnp.float32)
        mixed.append(
            (first[None, :] * first_out + second[None, :] * second_out).T.astype(jnp.bfloat16)
        )
        cot_cols = cotangent[step].T.astype(jnp.float32)
        partial_dots = jnp.stack(
            [jnp.sum(cot_cols * first_out, axis=0), jnp.sum(cot_cols * second_out, axis=0)]
        )
        gate_dots = taken_together(partial_dots, REP)
        delta = (gate_dots[0] - gate_dots[1]) * first * second
        logit_grad = delta[:, None] * (
            hits[:, 0].astype(jnp.float32) - hits[:, 1].astype(jnp.float32)
        )
        router_acc = router_acc + jnp.dot(
            tokens[step].astype(jnp.float32).T, logit_grad, precision=lax.Precision.HIGHEST
        )
        router_in = jnp.dot(logit_grad, router_wide.T, precision=lax.Precision.HIGHEST)
        expert_cots = deliver(cotangent[step], source_row, filled, slot_gate)
        hidden_grad = contract_last(expert_cots, down_w)
        gate_pre_grad = (
            hidden_grad * pre_up * (gate_sig * (1.0 + pre_gate * (1.0 - gate_sig)))
        ).astype(jnp.bfloat16)
        up_pre_grad = (hidden_grad * gate_act).astype(jnp.bfloat16)
        down_acc = down_acc + contract_first(hidden, expert_cots)
        gate_acc = gate_acc + contract_first(expert_rows, gate_pre_grad)
        up_acc = up_acc + contract_first(expert_rows, up_pre_grad)
        input_cols = sum_by_axis(
            (contract_last(gate_w, gate_pre_grad) + contract_last(up_w, up_pre_grad)).astype(
                jnp.bfloat16
            ),
            (("rep_0", "rep_1"), "rep_2"),
            0,
        ).astype(jnp.bfloat16)
        returned_grad = collect(input_cols)
        grad_cols = jnp.take(returned_grad, slots[:, 0], axis=1).astype(jnp.float32)
        grad_cols = grad_cols + jnp.take(returned_grad, slots[:, 1], axis=1).astype(jnp.float32)
        token_grad.append((grad_cols + router_in.T).T.astype(jnp.bfloat16))
    router_total = taken_together(router_acc, "ep")
    return (
        jnp.stack(mixed),
        jnp.stack(token_grad),
        gate_acc.astype(jnp.bfloat16)[None],
        up_acc.astype(jnp.bfloat16)[None],
        down_acc.astype(jnp.bfloat16)[None],
        router_total,
    )


def solution(mesh):
    split = Mesh(mesh.devices.reshape(4, 4, 2, mesh.shape["ep"]), ("rep_0", "rep_1", "rep_2", "ep"))
    in_specs = (
        P(None, "ep", REP),
        P(None, "ep", None),
        P(REP, None),
        P("ep", None, REP),
        P("ep", None, REP),
        P("ep", REP, None),
        P(None, "ep", REP),
    )
    out_specs = (
        P(None, "ep", REP),
        P(None, "ep", REP),
        P("ep", None, REP),
        P("ep", None, REP),
        P("ep", REP, None),
        P(REP, None),
    )
    return jax.shard_map(
        shards, mesh=split, in_specs=in_specs, out_specs=out_specs, check_vma=False
    )
```

profile of v0, /device:TPU:32, one launch (start us, length us, event | category | flops | bytes accessed | tf_op | source)
XLA Modules:
  0.0 662.4 jit_solution(15481597892796571032)
XLA Ops:
  12.3 20.5 %all_to_all.156 = bf16[8,48,128]{2,1,0:T(8,128)(2,1)} all-to-all(bf16[8,48,128]{2,1,0:T(8,128)(2,1)S(1)} %bitcast.283), channel_id=1, replica_groups=mesh['rep_0'=4,'rep_1'=4,'rep_2'=2,'ep'=8] {'ep'}, dimensions={0} | all-to-all | bytes 196608 | tf_op jit(solution)/shard_map/all_to_all | solution.py:80
  34.8 13.4 %all_to_all.157 = bf16[8,48,128]{2,1,0:T(8,128)(2,1)} all-to-all(bf16[8,48,128]{2,1,0:T(8,128)(2,1)S(1)} %bitcast.284), channel_id=1, replica_groups=mesh['rep_0'=4,'rep_1'=4,'rep_2'=2,'ep'=8] {'ep'}, dimensions={0} | all-to-all | bytes 196608 | tf_op jit(solution)/shard_map/all_to_all | solution.py:80
  48.4 47.2 %all-gather.5.cloned.1.call-done = bf16[384,4096]{1,0:T(8,128)(2,1)} async-done(((bf16[384,128]{1,0:T(8,128)(2,1)}), bf16[384,4096]{1,0:T(8,128)(2,1)}) %all-gather.5.cloned.1.call-update) | async-done | bytes 3145744 | tf_op jit(solution)/shard_map/all_gather | solution.py:83
  104.2 6.1 reshape_reshape.12
  119.5 43.7 %all-gather.7.cloned.1.call-done = bf16[384,4096]{1,0:T(8,128)(2,1)} async-done(((bf16[384,128]{1,0:T(8,128)(2,1)}), bf16[384,4096]{1,0:T(8,128)(2,1)}) %all-gather.7.cloned.1.call-update) | async-done | bytes 3145744 | tf_op jit(solution)/shard_map/all_gather | solution.py:83
  168.2 5.6 all-to-all-start
  187.9 6.1 reshape_reshape.13
  198.0 10.4 %all_to_all.158 = bf16[2,16,128,384]{2,1,3,0:T(8,128)(2,1)} all-to-all(bf16[2,16,128,384]{2,1,3,0:T(8,128)(2,1)} %bitcast.267), channel_id=1, replica_groups=mesh['rep_0'=4,'rep_1'=4,'rep_2'=2,'ep'=8] {'rep_2'}, dimensions={0} | all-to-all | bytes 6291456 | tf_op jit(solution)/shard_map/all_to_all | solution.py:31
  208.3 7.8 %all-to-all-start.3 = ((bf16[16,128,384]{1,2,0:T(8,128)(2,1)}), bf16[16,128,384]{1,2,0:T(8,128)(2,1)}, u32[]{:S(2)}, u32[]{:S(2)}) async-start(bf16[16,128,384]{1,2,0:T(8,128)(2,1)} %copy.78), calls=%async_computation.3 | async-start | bytes 3145728 | tf_op jit(solution)/shard_map/all_to_all | solution.py:39
  223.1 30.0 %all-to-all-done.3 = bf16[16,128,384]{1,2,0:T(8,128)(2,1)} async-done(((bf16[16,128,384]{1,2,0:T(8,128)(2,1)}), bf16[16,128,384]{1,2,0:T(8,128)(2,1)}, u32[]{:S(2)}, u32[]{:S(2)}) %all-to-all-start.3) | async-done | bytes 1572896 | tf_op jit(solution)/shard_map/all_to_all | solution.py:39
  253.1 5.5 all-to-all-start.7
  262.5 32.1 %all-to-all-done.7 = bf16[16,128,384]{1,2,0:T(8,128)(2,1)} async-done(((bf16[16,128,384]{1,2,0:T(8,128)(2,1)}), bf16[16,128,384]{1,2,0:T(8,128)(2,1)}, u32[]{:S(2)}, u32[]{:S(2)}) %all-to-all-start.7) | async-done | bytes 1572896 | tf_op jit(solution)/shard_map/all_to_all | solution.py:39
  294.5 7.8 %all-to-all-start.4 = ((bf16[128,8,48]{0,2,1:T(8,128)(2,1)}), bf16[128,8,48]{0,2,1:T(8,128)(2,1)S(1)}, u32[]{:S(2)}, u32[]{:S(2)}) async-start(bf16[128,8,48]{0,2,1:T(8,128)(2,1)} %bitcast.15), calls=%async_computation.4 | async-start | bytes 196608 | tf_op jit(solution)/shard_map/all_to_all | solution.py:88
  304.7 8.2 %all-to-all-done.4 = bf16[128,8,48]{0,2,1:T(8,128)(2,1)S(1)} async-done(((bf16[128,8,48]{0,2,1:T(8,128)(2,1)}), bf16[128,8,48]{0,2,1:T(8,128)(2,1)S(1)}, u32[]{:S(2)}, u32[]{:S(2)}) %all-to-all-start.4) | async-done | bytes 98336 | tf_op jit(solution)/shard_map/all_to_all | solution.py:88
  317.7 8.9 %all-to-all-done.8 = bf16[128,8,48]{0,2,1:T(8,128)(2,1)S(1)} async-done(((bf16[128,8,48]{0,2,1:T(8,128)(2,1)}), bf16[128,8,48]{0,2,1:T(8,128)(2,1)S(1)}, u32[]{:S(2)}, u32[]{:S(2)}) %all-to-all-start.8) | async-done | bytes 98336 | tf_op jit(solution)/shard_map/all_to_all | solution.py:88
  328.8 6.1 all-to-all-start.18
  335.0 6.5 all-to-all-done.18
  342.0 14.1 %all_to_all.159 = bf16[8,48,128]{2,1,0:T(8,128)(2,1)} all-to-all(bf16[8,48,128]{2,1,0:T(8,128)(2,1)S(1)} %bitcast.281), channel_id=1, replica_groups=mesh['rep_0'=4,'rep_1'=4,'rep_2'=2,'ep'=8] {'ep'}, dimensions={0} | all-to-all | bytes 196608 | tf_op jit(solution)/shard_map/all_to_all | solution.py:80
  362.5 6.6 all-to-all-done.13
  369.5 14.3 %all_to_all.160 = bf16[8,48,128]{2,1,0:T(8,128)(2,1)} all-to-all(bf16[8,48,128]{2,1,0:T(8,128)(2,1)S(1)} %bitcast.282), channel_id=1, replica_groups=mesh['rep_0'=4,'rep_1'=4,'rep_2'=2,'ep'=8] {'ep'}, dimensions={0} | all-to-all | bytes 196608 | tf_op jit(solution)/shard_map/all_to_all | solution.py:80
  384.2 33.7 %all-gather.11.cloned.1.call-done = bf16[384,4096]{1,0:T(8,128)(2,1)} async-done(((bf16[384,128]{1,0:T(8,128)(2,1)}), bf16[384,4096]{1,0:T(8,128)(2,1)}) %all-gather.11.cloned.1.call-update) | async-done | bytes 3145744 | tf_op jit(solution)/shard_map/all_gather | solution.py:83
  425.5 6.1 reshape_reshape.15
  440.9 44.8 %all-gather.9.cloned.1.call-done = bf16[384,4096]{1,0:T(8,128)(2,1)} async-done(((bf16[384,128]{1,0:T(8,128)(2,1)}), bf16[384,4096]{1,0:T(8,128)(2,1)}) %all-gather.9.cloned.1.call-update) | async-done | bytes 3145744 | tf_op jit(solution)/shard_map/all_gather | solution.py:83
  493.3 8.1 %all-to-all-start.19 = ((f32[8,128,8]{1,2,0:T(8,128)}), f32[8,128,8]{1,2,0:T(8,128)S(1)}, u32[]{:S(2)}, u32[]{:S(2)}) async-start(f32[8,128,8]{1,2,0:T(8,128)} %broadcast_in_dim.184), calls=%async_computation.19 | async-start | bytes 65536 | tf_op jit(solution)/shard_map/all_to_all | solution.py:13
  501.3 5.5 fusion.5
  511.9 6.1 reshape_reshape.14
  521.9 10.3 %all_to_all.161 = bf16[2,16,128,384]{2,1,3,0:T(8,128)(2,1)} all-to-all(bf16[2,16,128,384]{2,1,3,0:T(8,128)(2,1)} %bitcast.268), channel_id=1, replica_groups=mesh['rep_0'=4,'rep_1'=4,'rep_2'=2,'ep'=8] {'rep_2'}, dimensions={0} | all-to-all | bytes 6291456 | tf_op jit(solution)/shard_map/all_to_all | solution.py:31
  544.6 29.9 %all-to-all-done.16 = bf16[16,128,384]{1,2,0:T(8,128)(2,1)S(1)} async-done(((bf16[16,128,384]{1,2,0:T(8,128)(2,1)}), bf16[16,128,384]{1,2,0:T(8,128)(2,1)S(1)}, u32[]{:S(2)}, u32[]{:S(2)}) %all-to-all-start.16) | async-done | bytes 1572896 | tf_op jit(solution)/shard_map/all_to_all | solution.py:39
  575.6 5.8 all-to-all-start.11
  595.8 21.4 %all-to-all-done.11 = bf16[16,128,384]{1,2,0:T(8,128)(2,1)S(1)} async-done(((bf16[16,128,384]{1,2,0:T(8,128)(2,1)}), bf16[16,128,384]{1,2,0:T(8,128)(2,1)S(1)}, u32[]{:S(2)}, u32[]{:S(2)}) %all-to-all-start.11) | async-done | bytes 1572896 | tf_op jit(solution)/shard_map/all_to_all | solution.py:39
  617.2 9.6 %all-to-all-start.17 = ((bf16[128,8,48]{0,2,1:T(8,128)(2,1)}), bf16[128,8,48]{0,2,1:T(8,128)(2,1)S(1)}, u32[]{:S(2)}, u32[]{:S(2)}) async-start(bf16[128,8,48]{0,2,1:T(8,128)(2,1)} %bitcast.65), calls=%async_computation.17 | async-start | bytes 196608 | tf_op jit(solution)/shard_map/all_to_all | solution.py:88
  642.3 5.9 fusion.7
  (162 shorter events, 159.9 us)
Async XLA Ops:
  7.2 94.3 %copy-start = (bf16[1,256,4096]{2,1,0:T(8,128)(2,1)S(1)}, bf16[1,256,4096]{2,1,0:T(8,128)(2,1)}, u32[]{:S(2)}) copy-start(bf16[1,256,4096]{2,1,0:T(8,128)(2,1)} %param.16) | copy-start | bytes 6291460
  7.2 41.0 %copy-start.11 = (bf16[2,128,128]{2,1,0:T(8,128)(2,1)S(1)}, bf16[2,128,128]{2,1,0:T(8,128)(2,1)}, u32[]{:S(2)}) copy-start(bf16[2,128,128]{2,1,0:T(8,128)(2,1)} %param.11) | copy-start | bytes 196612
  7.2 41.0 %copy-start.14 = (bf16[128,8]{0,1:T(8,128)(2,1)S(1)}, bf16[128,8]{0,1:T(8,128)(2,1)}, u32[]{:S(2)}) copy-start(bf16[128,8]{0,1:T(8,128)(2,1)} %param.13) | copy-start | bytes 6148
  7.2 88.4 %all-gather.5.cloned.1.call-start = ((), (), s32[]{:S(2)}) async-start(), calls=%async_computation.20 | async-start | bytes 3244032 | tf_op jit(solution)/shard_map/all_gather | solution.py:83
  32.8 130.4 %all-gather.7.cloned.1.call-start = ((), (), s32[]{:S(2)}) async-start(), calls=%async_computation.21 | async-start | bytes 3244032 | tf_op jit(solution)/shard_map/all_gather | solution.py:83
  95.6 3.7 copy-start.3
  95.6 4.1 copy-start.7
  99.7 1.8 copy-start.15
  114.3 53.2 %all-to-all-start.2 = ((bf16[2,16,128,384]{2,1,3,0:T(8,128)(2,1)}), bf16[2,16,128,384]{2,1,3,0:T(8,128)(2,1)}, u32[]{:S(2)}, u32[]{:S(2)}) async-start(bf16[2,16,128,384]{2,1,3,0:T(8,128)(2,1)} %bitcast.266), calls=%async_computation.2 | async-start | bytes 6291456 | tf_op jit(solution)/shard_map/all_to_all | solution.py:31
  168.2 29.7 %all-to-all-start = ((f32[32,2,128,8]{2,3,1,0:T(8,128)}), f32[32,2,128,8]{2,3,1,0:T(8,128)S(1)}, u32[]{:S(2)}, u32[]{:S(2)}) async-start(f32[32,2,128,8]{2,3,1,0:T(8,128)} %broadcast_in_dim.162), calls=%async_computation | async-start | bytes 524288 | tf_op jit(solution)/shard_map/all_to_all | solution.py:13
  208.3 44.8 %all-to-all-start.3 = ((bf16[16,128,384]{1,2,0:T(8,128)(2,1)}), bf16[16,128,384]{1,2,0:T(8,128)(2,1)}, u32[]{:S(2)}, u32[]{:S(2)}) async-start(bf16[16,128,384]{1,2,0:T(8,128)(2,1)} %copy.78), calls=%async_computation.3 | async-start | bytes 3145728 | tf_op jit(solution)/shard_map/all_to_all | solution.py:39
  220.1 38.5 %copy-start.12 = (bf16[2,128,128]{2,1,0:T(8,128)(2,1)S(1)}, bf16[2,128,128]{2,1,0:T(8,128)(2,1)}, u32[]{:S(2)}) copy-start(bf16[2,128,128]{2,1,0:T(8,128)(2,1)} %param.17) | copy-start | bytes 196612
  220.1 40.0 %copy-start.13 = (s32[2,128,2]{1,2,0:T(2,128)S(1)}, s32[2,128,2]{1,2,0:T(2,128)}, u32[]{:S(2)}) copy-start(s32[2,128,2]{1,2,0:T(2,128)} %param.12) | copy-start | bytes 6148
  253.1 41.4 %all-to-all-start.7 = ((bf16[16,128,384]{1,2,0:T(8,128)(2,1)}), bf16[16,128,384]{1,2,0:T(8,128)(2,1)}, u32[]{:S(2)}, u32[]{:S(2)}) async-start(bf16[16,128,384]{1,2,0:T(8,128)(2,1)} %copy.84), calls=%async_computation.7 | async-start | bytes 3145728 | tf_op jit(solution)/shard_map/all_to_all | solution.py:39
  294.5 18.3 %all-to-all-start.4 = ((bf16[128,8,48]{0,2,1:T(8,128)(2,1)}), bf16[128,8,48]{0,2,1:T(8,128)(2,1)S(1)}, u32[]{:S(2)}, u32[]{:S(2)}) async-start(bf16[128,8,48]{0,2,1:T(8,128)(2,1)} %bitcast.15), calls=%async_computation.4 | async-start | bytes 196608 | tf_op jit(solution)/shard_map/all_to_all | solution.py:88
  312.9 13.7 %all-to-all-start.8 = ((bf16[128,8,48]{0,2,1:T(8,128)(2,1)}), bf16[128,8,48]{0,2,1:T(8,128)(2,1)S(1)}, u32[]{:S(2)}, u32[]{:S(2)}) async-start(bf16[128,8,48]{0,2,1:T(8,128)(2,1)} %bitcast.34), calls=%async_computation.8 | async-start | bytes 196608 | tf_op jit(solution)/shard_map/all_to_all | solution.py:88
  328.8 12.7 %all-to-all-start.18 = ((f32[32,2,128]{2,1,0:T(2,128)}), f32[32,2,128]{2,1,0:T(2,128)S(1)}, u32[]{:S(2)}, u32[]{:S(2)}) async-start(f32[32,2,128]{2,1,0:T(2,128)} %broadcast_in_dim.180), calls=%async_computation.18 | async-start | bytes 65536 | tf_op jit(solution)/shard_map/all_to_all | solution.py:13
  335.0 82.9 %all-gather.11.cloned.1.call-start = ((), (), s32[]{:S(2)}) async-start(), calls=%async_computation.23 | async-start | bytes 3244032 | tf_op jit(solution)/shard_map/all_gather | solution.py:83
  358.2 10.9 %all-to-all-start.13 = ((f32[32,2,128]{2,1,0:T(2,128)}), f32[32,2,128]{2,1,0:T(2,128)S(1)}, u32[]{:S(2)}, u32[]{:S(2)}) async-start(f32[32,2,128]{2,1,0:T(2,128)} %broadcast_in_dim.178), calls=%async_computation.13 | async-start | bytes 65536 | tf_op jit(solution)/shard_map/all_to_all | solution.py:13
  362.5 123.2 %all-gather.9.cloned.1.call-start = ((), (), s32[]{:S(2)}) async-start(), calls=%async_computation.22 | async-start | bytes 3244032 | tf_op jit(solution)/shard_map/all_gather | solution.py:83
  417.9 3.3 copy-start.5
  435.5 57.2 %all-to-all-start.15 = ((bf16[2,16,128,384]{2,1,3,0:T(8,128)(2,1)}), bf16[2,16,128,384]{2,1,3,0:T(8,128)(2,1)}, u32[]{:S(2)}, u32[]{:S(2)}) async-start(bf16[2,16,128,384]{2,1,3,0:T(8,128)(2,1)} %bitcast.265), calls=%async_computation.15 | async-start | bytes 6291456 | tf_op jit(solution)/shard_map/all_to_all | solution.py:31
  485.7 3.2 copy-start.6
  489.0 12.4 %copy-start.9 = (bf16[1,4096,256]{2,1,0:T(8,128)(2,1)S(1)}, bf16[1,4096,256]{2,1,0:T(8,128)(2,1)}, u32[]{:S(2)}) copy-start(bf16[1,4096,256]{2,1,0:T(8,128)(2,1)} %param.15) | copy-start | bytes 6291460
  493.3 28.6 %all-to-all-start.19 = ((f32[8,128,8]{1,2,0:T(8,128)}), f32[8,128,8]{1,2,0:T(8,128)S(1)}, u32[]{:S(2)}, u32[]{:S(2)}) async-start(f32[8,128,8]{1,2,0:T(8,128)} %broadcast_in_dim.184), calls=%async_computation.19 | async-start | bytes 65536 | tf_op jit(solution)/shard_map/all_to_all | solution.py:13
  532.3 42.2 %all-to-all-start.16 = ((bf16[16,128,384]{1,2,0:T(8,128)(2,1)}), bf16[16,128,384]{1,2,0:T(8,128)(2,1)S(1)}, u32[]{:S(2)}, u32[]{:S(2)}) async-start(bf16[16,128,384]{1,2,0:T(8,128)(2,1)} %copy.91), calls=%async_computation.16 | async-start | bytes 3145728 | tf_op jit(solution)/shard_map/all_to_all | solution.py:39
  575.6 41.5 %all-to-all-start.11 = ((bf16[16,128,384]{1,2,0:T(8,128)(2,1)}), bf16[16,128,384]{1,2,0:T(8,128)(2,1)S(1)}, u32[]{:S(2)}, u32[]{:S(2)}) async-start(bf16[16,128,384]{1,2,0:T(8,128)(2,1)} %copy.87), calls=%async_computation.11 | async-start | bytes 3145728 | tf_op jit(solution)/shard_map/all_to_all | solution.py:39
  583.0 3.3 copy-start.4
  586.4 1.9 copy-start.2
  617.2 20.1 %all-to-all-start.17 = ((bf16[128,8,48]{0,2,1:T(8,128)(2,1)}), bf16[128,8,48]{0,2,1:T(8,128)(2,1)S(1)}, u32[]{:S(2)}, u32[]{:S(2)}) async-start(bf16[128,8,48]{0,2,1:T(8,128)(2,1)} %bitcast.65), calls=%async_computation.17 | async-start | bytes 196608 | tf_op jit(solution)/shard_map/all_to_all | solution.py:88
  637.3 15.6 %all-to-all-start.12 = ((bf16[128,8,48]{0,2,1:T(8,128)(2,1)}), bf16[128,8,48]{0,2,1:T(8,128)(2,1)S(1)}, u32[]{:S(2)}, u32[]{:S(2)}) async-start(bf16[128,8,48]{0,2,1:T(8,128)(2,1)} %bitcast.47), calls=%async_computation.12 | async-start | bytes 196608 | tf_op jit(solution)/shard_map/all_to_all | solution.py:88
  642.3 13.2 %copy-start.1 = (bf16[1,256,4096]{2,1,0:T(8,128)(2,1)S(1)}, bf16[1,256,4096]{2,1,0:T(8,128)(2,1)}, u32[]{:S(2)}) copy-start(bf16[1,256,4096]{2,1,0:T(8,128)(2,1)} %param.16) | copy-start | bytes 6291460
  (2 other events, 2.7 us)
Sparse Core Ops, SparseCore 0:
  32.9 62.6 all-gather.4
  97.4 65.8 all-gather.6
  356.2 61.5 all-gather.10
  419.5 66.1 all-gather.8
where the time goes:
time: 673 us; the launch traced here: 662 us
  waiting for transfers between devices  321 us (48%)
  starting transfers between devices  84.9 us (13%)
  blocking collectives  83 us (12%)
  local copies, waits for them, and re-layouts  69.5 us (10%)
  matrix products  60.5 us (9%)
  other arithmetic  28.9 us (4%)
  between operations  14.7 us (2%)
    all_gather x4, waiting for transfers between devices, deliver(): result = lax.all_gather(moved, REP, axis=1, tiled=True)  169 us
    all_to_all x4, waiting for transfers between devices, sum_by_axis(): lax.all_to_all(nearer.astype(jnp.bfloat16), far, split_axis=0, concat_axi...  113 us
    all_to_all x4, blocking collectives, deliver(): lax.all_to_all(pack(rows, source_row, filled, scale), 'ep', split_axis=0,...  62.3 us
    another operation x8, local copies, waits for them, and re-layouts, split_up(): array.reshape(*dims[:dim], devices, dims[dim] // devices, *dims[dim + 1:])  40.2 us
    all_to_all x4, starting transfers between devices, collect(): lax.all_to_all(columns, 'ep', split_axis=1, concat_axis=1, tiled=True)  25.7 us
    all_to_all x4, waiting for transfers between devices, collect(): lax.all_to_all(columns, 'ep', split_axis=1, concat_axis=1, tiled=True)  24.9 us
    all_to_all x4, starting transfers between devices, sum_by_axis(): lax.all_to_all(nearer.astype(jnp.bfloat16), far, split_axis=0, concat_axi...  24.4 us
    all_to_all x4, starting transfers between devices, copy_for_each(): lax.all_to_all(jnp.broadcast_to(array[None], (devices, *array.shape)), ax...  24.1 us
  transfers between devices with their start and end apart: 18, of which 14 were waited for; matrix products, arithmetic and copies ran while one was open for 22% of the time, Pallas kernels for 0%

commit v1 on v0

v1 whole, which is shorter than its diff:
```python
import jax
import jax.numpy as jnp
from jax import lax
from jax.experimental import pallas as pl
from jax.experimental.pallas import tpu as pltpu
from jax.sharding import Mesh
from jax.sharding import PartitionSpec as P

MESH = pl.DeviceIdType.MESH
REP = ("zl", "x", "c")
EP = ("zh", "y")
F32 = jnp.float32
BF = jnp.bfloat16
CAP = 48
ROWS = 384
BLK = 128
HID = 256
PEERS = [(dz, dy) for dz in range(2) for dy in range(4) if dz or dy]


def rem(value, n):
    return lax.rem(value, jnp.int32(n))


def wait(ref, sem):
    pltpu.make_async_copy(ref, ref, sem).wait()


def dot(a, b):
    return jnp.dot(a, b, preferred_element_type=F32)


def dot_tn(a, b):
    return lax.dot_general(a, b, (((0,), (0,)), ((), ())), preferred_element_type=F32)


def dot_nt(a, b):
    return lax.dot_general(a, b, (((1,), (1,)), ((), ())), preferred_element_type=F32)


def iota(rows, lanes, dim):
    return lax.broadcasted_iota(jnp.int32, (rows, lanes), dim).astype(F32)


def to_row(col):
    n = col.shape[0]
    return jnp.sum(jnp.where(iota(n, BLK, 0) == iota(n, BLK, 1), col, 0.0), axis=0, keepdims=True)


def to_col(row, n):
    return jnp.sum(jnp.where(iota(n, BLK, 0) == iota(n, BLK, 1), row, 0.0), axis=1, keepdims=True)


def tile_of(rows):
    sub = iota(8, BLK, 0)
    return jnp.where(sub == 0.0, rows[0], 0.0) + jnp.where(sub == 1.0, rows[1], 0.0)


def sigmoid(v):
    return 1.0 / (1.0 + jnp.exp(-v))


def kernel(
    tok, cot, ids, rwt, wg_h, wu_h, wd_h,
    mixed, tgrad, gg_h, ug_h, dg_h, rg,
    G, wg, wu, wd, WgH, WuH, WdH, snd, AG, AU, HG, HC, PG, PU, HS, gcol, dcol,
    Pt, FX, XL, XR, zs, zr, zo, fin, ret, slots, gates, dmat, arS, arR, gts, gtr, dts, dtr, rgs, rgr,
    w_l, w_s, w_r, a_s, a_r, z_s, z_r, x_s, xl_r, xr_r, f_r, d_s, d_r, h_s, h_r,
    rx_s, rf_r, rl_r, rr_r, rz_s, rz_r, b_s, b_r, ar_s, ar_r, gt_s, gt_r, dt_s, dt_r, rg_s, rg_r, o_s,
):
    zl = lax.axis_index("zl")
    x = lax.axis_index("x")
    c = lax.axis_index("c")
    zh = lax.axis_index("zh")
    y = lax.axis_index("y")
    right, left, far = rem(x + 1, 4), rem(x + 3, 4), rem(x + 2, 4)
    e = zh * 4 + y
    oc = 1 - c
    r = zl * 8 + x * 2 + c

    def send(src, dst, ss, rs, dev):
        pltpu.make_async_remote_copy(
            src_ref=src, dst_ref=dst, send_sem=ss, recv_sem=rs, device_id=dev, device_id_type=MESH
        ).start()

    def lanes(index, width=BLK):
        return pl.ds(pl.multiple_of(index * width, width), width)

    def feat(zl_, x_, c_):
        return zl_ * 8 + x_ * 2 + c_

    def col(arr, zl_, x_):
        return G.at[arr, :, lanes(feat(zl_, x_, c))]

    def cap(index):
        return pl.ds(pl.multiple_of(index * CAP, 16), CAP)

    mine = lanes(c, HID)

    pltpu.make_async_copy(wg_h, wg, w_l.at[0]).start()
    pltpu.make_async_copy(wu_h, wu, w_l.at[1]).start()
    pltpu.make_async_copy(wd_h, wd, w_l.at[2]).start()

    @pl.loop(0, 16)
    def _(b):
        at = feat(b // 4, b % 4, c)
        pltpu.make_async_copy(wg_h.at[lanes(at), :], WgH.at[lanes(b), mine], w_l.at[3]).start()
        pltpu.make_async_copy(wu_h.at[lanes(at), :], WuH.at[lanes(b), mine], w_l.at[4]).start()
        pltpu.make_async_copy(wd_h.at[:, lanes(at)], WdH.at[mine, lanes(b)], w_l.at[5]).start()

    barrier = pltpu.get_barrier_semaphore()
    pl.semaphore_signal(barrier, inc=1, device_id={"c": oc}, device_id_type=MESH)
    for j in range(1, 4):
        pl.semaphore_signal(barrier, inc=1, device_id={"x": rem(x + j, 4)}, device_id_type=MESH)
        pl.semaphore_signal(barrier, inc=1, device_id={"zl": rem(zl + j, 4)}, device_id_type=MESH)
    for dz, dy in PEERS:
        dev = {"zh": rem(zh + dz, 2), "y": rem(y + dy, 4)}
        pl.semaphore_signal(barrier, inc=1, device_id=dev, device_id_type=MESH)

    sub, lane = iota(BLK, BLK, 0), iota(BLK, BLK, 1)

    def hits(m):
        both = ids[m].astype(F32)
        first, second = both[:, 0:1], both[:, 1:2]
        return first, second, jnp.where(first == lane, 1.0, 0.0), jnp.where(second == lane, 1.0, 0.0)

    spread = []
    for m in range(2):
        first, second, h0, h1 = hits(m)
        tri = jnp.where(lane < sub, 1.0, 0.0).astype(BF)
        before = dot(tri, (h0 + h1).astype(BF))
        s0 = first * float(CAP) + jnp.sum(h0 * before, axis=1, keepdims=True)
        s1 = second * float(CAP) + jnp.sum(h1 * before, axis=1, keepdims=True)
        slots[m, 0] = jnp.broadcast_to(s0, (BLK, BLK))
        slots[m, 1] = jnp.broadcast_to(s1, (BLK, BLK))
        at = iota(ROWS, BLK, 0)
        match = jnp.where((at == to_row(s0)) | (at == to_row(s1)), 1.0, 0.0).astype(BF)
        snd[2 * m] = dot(match, tok[m]).astype(BF)
        snd[2 * m + 1] = dot(match, cot[m]).astype(BF)
        diff = dot((h0 - h1).astype(BF), rwt[...])
        dmat[m] = diff
        spread.append(to_row(jnp.sum(tok[m].astype(F32) * diff, axis=1, keepdims=True)))
    arS[0, 0] = tile_of(spread)
    for arr in range(4):
        G[arr, cap(e), lanes(r)] = snd[arr, cap(e), :]

    pl.semaphore_wait(barrier, 14)

    for arr in range(4):
        for dz, dy in PEERS:
            tz, ty = rem(zh + dz, 2), rem(y + dy, 4)
            send(snd.at[arr, cap(tz * 4 + ty), :], G.at[arr, cap(e), lanes(r)],
                 a_s.at[arr], a_r.at[arr], {"zh": tz, "y": ty})

    def ar_core(k):
        send(arS.at[k, 0], arR.at[k, 0], ar_s.at[k, 0], ar_r.at[k, 0], {"c": oc})

    def ar_x(k):
        wait(arR.at[k, 0], ar_r.at[k, 0])
        arS[k, 1] = arS[k, 0] + arR[k, 0]
        for j in range(1, 4):
            send(arS.at[k, 1], arR.at[k, j], ar_s.at[k, 1], ar_r.at[k, j], {"x": rem(x + j, 4)})

    def ar_z(k):
        total = arS[k, 1]
        for j in range(1, 4):
            wait(arR.at[k, j], ar_r.at[k, j])
            total = total + arR[k, j]
        arS[k, 2] = total
        for j in range(1, 4):
            send(arS.at[k, 2], arR.at[k, 3 + j], ar_s.at[k, 2], ar_r.at[k, 3 + j], {"zl": rem(zl + j, 4)})

    def ar_end(k):
        total = arS[k, 2]
        for j in range(1, 4):
            wait(arR.at[k, 3 + j], ar_r.at[k, 3 + j])
            total = total + arR[k, 3 + j]
        return total

    ar_core(0)

    @pl.loop(0, 16)
    def _(b):
        at = feat(b // 4, b % 4, oc)
        send(wg_h.at[lanes(at), :], WgH.at[lanes(b), mine], w_s.at[0], w_r.at[0], {"c": oc})
        send(wu_h.at[lanes(at), :], WuH.at[lanes(b), mine], w_s.at[1], w_r.at[1], {"c": oc})
        send(wd_h.at[:, lanes(at)], WdH.at[mine, lanes(b)], w_s.at[2], w_r.at[2], {"c": oc})

    def spread_block(arr, zl_, j):
        here = col(arr, zl_, x)
        send(here, here, x_s.at[arr], xl_r.at[arr, j], {"x": right})
        send(here, here, x_s.at[arr], xr_r.at[arr, j], {"x": left})
        send(here, here, d_s.at[arr], d_r.at[arr], {"c": oc})

    def stage_a(arr):
        wait(snd.at[arr, 0:336, :], a_r.at[arr])
        here = col(arr, zl, x)
        for j in range(1, 4):
            send(here, here, z_s.at[arr], z_r.at[arr, j - 1], {"zl": rem(zl + 4 - j, 4)})
        spread_block(arr, zl, 0)

    def stage_b(arr):
        for j in range(1, 4):
            zj = rem(zl + j, 4)
            wait(col(arr, zj, x), z_r.at[arr, j - 1])
            spread_block(arr, zj, j)

    def stage_c(arr):
        for j in range(4):
            zj = rem(zl + j, 4)
            here = col(arr, zj, left)
            wait(here, xl_r.at[arr, j])
            if j % 2 == 0:
                send(here, here, x_s.at[arr], f_r.at[arr, j], {"x": right})
            send(here, here, d_s.at[arr], d_r.at[arr], {"c": oc})
            here = col(arr, zj, right)
            wait(here, xr_r.at[arr, j])
            if j % 2 == 1:
                send(here, here, x_s.at[arr], f_r.at[arr, j], {"x": left})
            send(here, here, d_s.at[arr], d_r.at[arr], {"c": oc})

    def stage_d(arr):
        for j in range(4):
            here = col(arr, rem(zl + j, 4), far)
            wait(here, f_r.at[arr, j])
            send(here, here, d_s.at[arr], d_r.at[arr], {"c": oc})

    def stage_e(arr):
        wait(G.at[arr, :, 0:2048], d_r.at[arr])

    def make_gates():
        total = ar_end(0)
        for m in range(2):
            diff = to_col(total[m : m + 1, :], BLK)
            gates[m, 0] = jnp.broadcast_to(sigmoid(diff), (BLK, BLK))
            gates[m, 1] = jnp.broadcast_to(sigmoid(-diff), (BLK, BLK))

        @pl.loop(0, 8)
        def _(ex):
            at = lane + (ex * CAP).astype(F32)
            rows = []
            for m in range(2):
                picked = jnp.where(slots[m, 0] == at, gates[m, 0], 0.0)
                picked = picked + jnp.where(slots[m, 1] == at, gates[m, 1], 0.0)
                rows.append(jnp.sum(picked, axis=0, keepdims=True))
            gts[ex] = tile_of(rows)

        gtr[e] = gts[e]
        for n, (dz, dy) in enumerate(PEERS):
            tz, ty = rem(zh + dz, 2), rem(y + dy, 4)
            send(gts.at[tz * 4 + ty], gtr.at[e], gt_s.at[0], gt_r.at[0], {"zh": tz, "y": ty})

    def take_gates():
        wait(gts.at[0:7], gt_r.at[0])

        @pl.loop(0, 8)
        def _(s):
            tile = gtr[s]
            for m in range(2):
                gcol[m, cap(s), :] = jnp.broadcast_to(to_col(tile[m : m + 1, :], CAP), (CAP, BLK))

    def pre(m):
        AG[...] = jnp.zeros_like(AG)
        AU[...] = jnp.zeros_like(AU)

        @pl.loop(0, 4)
        def _(k):
            rows = G[2 * m, :, lanes(k, 1024)]
            AG[...] += dot(rows, wg[lanes(k, 1024), :])
            AU[...] += dot(rows, wu[lanes(k, 1024), :])

    def back(m):
        HG[...] = jnp.zeros_like(HG)

        @pl.loop(0, 4)
        def _(k):
            HG[...] += dot_nt(G[2 * m + 1, :, lanes(k, 1024)], wd[:, lanes(k, 1024)])

        @pl.loop(0, 6)
        def _(i):
            rows = lanes(i, 64)
            pg, pu, hr = AG[rows, :], AU[rows, :], HG[rows, :]
            g = gcol[m, rows, 0:1]
            sig = sigmoid(pg)
            act = pg * sig
            hb = (act * pu).astype(BF)
            hw = hb.astype(F32)
            dcol[m, rows, :] = jnp.broadcast_to(jnp.sum(hw * hr, axis=1, keepdims=True), (64, BLK))
            hs = hr * g
            HC[m, rows, mine] = hb
            PG[m, rows, mine] = (hs * pu * (sig * (1.0 + pg * (1.0 - sig)))).astype(BF)
            PU[m, rows, mine] = (hs * act).astype(BF)
            HS[m, rows, :] = (hw * g).astype(BF)

        for n, buf in enumerate((HC, PG, PU)):
            send(buf.at[m, :, mine], buf.at[m, :, mine], h_s.at[m, n], h_r.at[m, n], {"c": oc})

    def part(a, zl_, x_):
        return Pt.at[a, :, lanes(zl_ * 4 + x_)]

    def first_sends(a, zp, parity, q):
        if parity == 0:
            send(part(a, zp, far), FX.at[a, zp], rx_s.at[a], rf_r.at[a, zp], {"x": right})
            send(part(a, zp, left), XR.at[a, zp], rx_s.at[a], rr_r.at[a, zp], {"x": left})
        else:
            send(part(a, zp, far), FX.at[a, zp], rx_s.at[a], rf_r.at[a, zp], {"x": left})
            send(part(a, zp, right), XL.at[a, zp], rx_s.at[a], rl_r.at[a, zp], {"x": right})

    def outs(m):
        a = 2 * m
        wait(HC.at[m, :, 0:HID], h_r.at[m, 0])

        @pl.loop(0, 2)
        def _(q):
            for parity in range(2):
                zp = q * 2 + parity
                Pt[a, :, lanes(zp, 512)] = dot(HC[m], WdH[:, lanes(zp, 512)]).astype(BF)
            for parity in range(2):
                first_sends(a, q * 2 + parity, parity, q)

    def ins(m):
        a = 2 * m + 1
        wait(PG.at[m, :, 0:HID], h_r.at[m, 1])
        wait(PU.at[m, :, 0:HID], h_r.at[m, 2])

        @pl.loop(0, 2)
        def _(q):
            for parity in range(2):
                zp = q * 2 + parity
                Pt[a, :, lanes(zp, 512)] = (
                    dot_nt(PG[m], WgH[lanes(zp, 512), :]) + dot_nt(PU[m], WuH[lanes(zp, 512), :])
                ).astype(BF)
            for parity in range(2):
                first_sends(a, q * 2 + parity, parity, q)

    def second_sends(a):
        for zp in range(4):
            wait(FX.at[a, zp], rf_r.at[a, zp])
            tx = right if zp % 2 == 0 else left
            where = lanes(zp * 4 + tx)
            Pt[a, :, where] = (Pt[a, :, where].astype(F32) + FX[a, zp].astype(F32)).astype(BF)
            if zp % 2 == 0:
                send(part(a, zp, tx), XL.at[a, zp], rx_s.at[a], rl_r.at[a, zp], {"x": right})
            else:
                send(part(a, zp, tx), XR.at[a, zp], rx_s.at[a], rr_r.at[a, zp], {"x": left})

    def third_sends(a):
        for j in (1, 2, 3, 0):
            zp = rem(zl + j, 4)
            wait(XL.at[a, zp], rl_r.at[a, zp])
            wait(XR.at[a, zp], rr_r.at[a, zp])
            total = Pt[a, :, lanes(zp * 4 + x)].astype(F32)
            total = total + XL[a, zp].astype(F32) + XR[a, zp].astype(F32)
            if j == 0:
                zo[a] = total
            else:
                zs[a, j - 1] = total.astype(BF)
                send(zs.at[a, j - 1], zr.at[a, j - 1], rz_s.at[a], rz_r.at[a, j - 1], {"zl": zp})

    def finish(a):
        total = zo[a]
        for j in range(3):
            wait(zr.at[a, j], rz_r.at[a, j])
            total = total + zr[a, j].astype(F32)
        fin[a] = total.astype(BF)
        ret[a, cap(e), :] = fin[a, cap(e), :]
        for dz, dy in PEERS:
            tz, ty = rem(zh + dz, 2), rem(y + dy, 4)
            send(fin.at[a, cap(tz * 4 + ty), :], ret.at[a, cap(e), :], b_s.at[a], b_r.at[a], {"zh": tz, "y": ty})

    def send_dots():
        @pl.loop(0, 8)
        def _(s):
            dts[s] = tile_of([to_row(dcol[m, cap(s), :]) for m in range(2)])

        dtr[e] = dts[e]
        for dz, dy in PEERS:
            tz, ty = rem(zh + dz, 2), rem(y + dy, 4)
            send(dts.at[tz * 4 + ty], dtr.at[e], dt_s.at[0], dt_r.at[0], {"zh": tz, "y": ty})

    def take_dots():
        wait(dts.at[0:7], dt_r.at[0])
        rows = []
        for m in range(2):
            total = jnp.zeros((BLK, BLK), F32)
            for ex in range(8):
                at = lane + float(ex * CAP)
                row = dtr[ex][m : m + 1, :]
                total = total + jnp.where(slots[m, 0] == at, row, 0.0) - jnp.where(slots[m, 1] == at, row, 0.0)
            rows.append(to_row(jnp.sum(total, axis=1, keepdims=True)))
        arS[1, 0] = tile_of(rows)
        ar_core(1)

    def weight_grads(lo, hi):
        @pl.loop(lo, hi)
        def _(i):
            at = lanes(i, 512)
            t0, t1 = G[0, :, at], G[2, :, at]
            wg[at, :] = (dot_tn(t0, PG[0, :, mine]) + dot_tn(t1, PG[1, :, mine])).astype(BF)
            wu[at, :] = (dot_tn(t0, PU[0, :, mine]) + dot_tn(t1, PU[1, :, mine])).astype(BF)
            wd[:, at] = (dot_tn(HS[0], G[1, :, at]) + dot_tn(HS[1], G[3, :, at])).astype(BF)

    stage_a(0)
    ar_x(0)
    stage_a(1)
    stage_b(0)
    ar_z(0)
    stage_a(2)
    stage_a(3)
    stage_b(1)
    make_gates()
    stage_c(0)
    stage_b(2)
    stage_c(1)
    stage_d(0)
    stage_b(3)
    stage_e(0)
    for k, buf in enumerate((wg, wu, wd)):
        wait(buf, w_l.at[k])
    for k, half in enumerate((WgH.at[:, 0:HID], WuH.at[:, 0:HID], WdH.at[0:HID, :])):
        wait(half, w_l.at[3 + k])
        wait(half, w_r.at[k])
    pre(0)
    stage_c(2)
    stage_d(1)
    stage_e(1)
    take_gates()
    back(0)
    outs(0)
    stage_c(3)
    ins(0)
    stage_d(2)
    stage_e(2)
    pre(1)
    second_sends(0)
    stage_d(3)
    stage_e(3)
    back(1)
    second_sends(1)
    outs(1)
    ins(1)
    send_dots()
    third_sends(0)
    third_sends(1)
    finish(0)
    take_dots()
    weight_grads(0, 4)
    second_sends(2)
    second_sends(3)
    ar_x(1)
    finish(1)
    weight_grads(4, 8)
    for k, (buf, out) in enumerate(((wg, gg_h), (wu, ug_h), (wd, dg_h))):
        pltpu.make_async_copy(buf, out, o_s.at[k]).start()
    ar_z(1)
    third_sends(2)
    third_sends(3)

    total = ar_end(1)
    share = jnp.zeros((BLK, BLK), F32)
    deltas = []
    for m in range(2):
        _, _, h0, h1 = hits(m)
        delta = to_col(total[m : m + 1, :], BLK) * gates[m, 0] * gates[m, 1]
        deltas.append(delta)
        share = share + lax.dot_general(
            delta * (h0 - h1), tok[m].astype(F32), (((0,), (0,)), ((), ())),
            preferred_element_type=F32, precision=lax.Precision.HIGHEST,
        )
    rgs[...] = share[0:8, :]
    for n, (dz, dy) in enumerate(PEERS):
        tz, ty = rem(zh + dz, 2), rem(y + dy, 4)
        send(rgs, rgr.at[n], rg_s.at[0], rg_r.at[n], {"zh": tz, "y": ty})
    finish(2)
    finish(3)

    for m in range(2):
        a = 2 * m
        wait(ret.at[a, 0:336, :], b_r.at[a])
        wait(ret.at[a + 1, 0:336, :], b_r.at[a + 1])
        one = jnp.zeros((BLK, BLK), F32)
        two = jnp.zeros((BLK, BLK), F32)
        grad = deltas[m] * dmat[m]
        for q in range(3):
            at = lane + float(q * BLK)
            p0 = jnp.where(slots[m, 0] == at, 1.0, 0.0)
            p1 = jnp.where(slots[m, 1] == at, 1.0, 0.0)
            rows = ret[a, q * BLK : (q + 1) * BLK, :]
            one = one + dot(p0.astype(BF), rows)
            two = two + dot(p1.astype(BF), rows)
            grad = grad + dot((p0 + p1).astype(BF), ret[a + 1, q * BLK : (q + 1) * BLK, :])
        mixed[m] = (gates[m, 0] * one + gates[m, 1] * two).astype(BF)
        tgrad[m] = grad.astype(BF)

    whole = rgs[...]
    for n in range(7):
        wait(rgr.at[n], rg_r.at[n])
        whole = whole + rgr[n]
    rg[...] = whole

    for arr in range(4):
        wait(snd.at[arr, 0:336, :], a_s.at[arr])
        wait(G.at[arr, :, 0:384], z_s.at[arr])
        wait(G.at[arr, :, 0:1536], x_s.at[arr])
        wait(G.at[arr, :, 0:2048], d_s.at[arr])
        wait(Pt.at[arr, :, 0:1536], rx_s.at[arr])
        wait(Pt.at[arr, :, 0:384], rz_s.at[arr])
        wait(fin.at[arr, 0:336, :], b_s.at[arr])
    for k, half in enumerate((WgH.at[:, 0:HID], WuH.at[:, 0:HID], WdH.at[0:HID, :])):
        wait(half, w_s.at[k])
    for m in range(2):
        for n, buf in enumerate((HC, PG, PU)):
            wait(buf.at[m, :, 0:HID], h_s.at[m, n])
    for k in range(2):
        wait(arR.at[k, 0], ar_s.at[k, 0])
        wait(arR.at[k, 1:4], ar_s.at[k, 1])
        wait(arR.at[k, 4:7], ar_s.at[k, 2])
    wait(gts.at[0:7], gt_s.at[0])
    wait(dts.at[0:7], dt_s.at[0])
    wait(rgr.at[0:7], rg_s.at[0])
    for k, (buf, out) in enumerate(((wg, gg_h), (wu, ug_h), (wd, dg_h))):
        pltpu.make_async_copy(buf, out, o_s.at[k]).wait()


def shards(tokens, expert_ids, router_weight, w_gate, w_up, w_down, cotangent):
    rwt = jnp.pad(router_weight.T, ((0, BLK - 8), (0, 0)))
    big = lambda *dims: pltpu.VMEM(dims, BF)
    wide = lambda *dims: pltpu.VMEM(dims, F32)
    dma = lambda *dims: pltpu.SemaphoreType.DMA(dims)
    vm = pl.BlockSpec(memory_space=pltpu.VMEM)
    anyw = pl.BlockSpec(memory_space=pl.ANY)
    D = 4096
    mixed, tgrad, gg, ug, dg, rg = pl.pallas_call(
        kernel,
        name="expert_layer",
        out_shape=(
            jax.ShapeDtypeStruct((2, BLK, BLK), BF),
            jax.ShapeDtypeStruct((2, BLK, BLK), BF),
            jax.ShapeDtypeStruct((D, HID), BF),
            jax.ShapeDtypeStruct((D, HID), BF),
            jax.ShapeDtypeStruct((HID, D), BF),
            jax.ShapeDtypeStruct((8, BLK), F32),
        ),
        in_specs=[vm, vm, vm, vm, anyw, anyw, anyw],
        out_specs=(vm, vm, anyw, anyw, anyw, vm),
        scratch_shapes=[
            big(4, ROWS, D), big(D, HID), big(D, HID), big(HID, D),
            big(2048, 512), big(2048, 512), big(512, 2048), big(4, ROWS, BLK),
            wide(ROWS, HID), wide(ROWS, HID), wide(ROWS, HID),
            big(2, ROWS, 512), big(2, ROWS, 512), big(2, ROWS, 512), big(2, ROWS, HID),
            wide(2, ROWS, BLK), wide(2, ROWS, BLK),
            big(4, ROWS, 2048), big(4, 4, ROWS, BLK), big(4, 4, ROWS, BLK), big(4, 4, ROWS, BLK),
            big(4, 3, ROWS, BLK), big(4, 3, ROWS, BLK), wide(4, ROWS, BLK), big(4, ROWS, BLK), big(4, ROWS, BLK),
            wide(2, 2, BLK, BLK), wide(2, 2, BLK, BLK), wide(2, BLK, BLK),
            wide(2, 3, 8, BLK), wide(2, 7, 8, BLK), wide(8, 8, BLK), wide(8, 8, BLK), wide(8, 8, BLK), wide(8, 8, BLK),
            wide(8, BLK), wide(7, 8, BLK),
            dma(6), dma(3), dma(3), dma(4), dma(4), dma(4), dma(4, 3), dma(4), dma(4, 4), dma(4, 4), dma(4, 4),
            dma(4), dma(4), dma(2, 3), dma(2, 3),
            dma(4), dma(4, 4), dma(4, 4), dma(4, 4), dma(4), dma(4, 3), dma(4), dma(4),
            dma(2, 3), dma(2, 7), dma(1), dma(1), dma(1), dma(1), dma(1), dma(7), dma(3),
        ],
        compiler_params=pltpu.CompilerParams(
            collective_id=0, has_side_effects=True, vmem_limit_bytes=64 * 1024 * 1024 - 65536 * 2
        ),
    )(tokens, cotangent, expert_ids, rwt, w_gate[0], w_up[0], w_down[0])
    return mixed, tgrad, gg[None], ug[None], dg[None], rg.T


def solution(mesh):
    split = Mesh(mesh.devices.reshape(4, 4, 2, 2, 4), REP + EP)
    in_specs = (
        P(None, EP, REP),
        P(None, EP, None),
        P(REP, None),
        P(EP, None, REP),
        P(EP, None, REP),
        P(EP, REP, None),
        P(None, EP, REP),
    )
    out_specs = (
        P(None, EP, REP),
        P(None, EP, REP),
        P(EP, None, REP),
        P(EP, None, REP),
        P(EP, REP, None),
        P(REP, None),
    )
    return jax.shard_map(shards, mesh=split, in_specs=in_specs, out_specs=out_specs, check_vma=False)
```

time: 673 us -> 174 us (0.26); the launches traced: 662 us -> 173 us
  waiting for transfers between devices: 321 us -> 0 us
  Pallas kernels: 0 us -> 159 us
  starting transfers between devices: 84.9 us -> 0 us
  blocking collectives: 83 us -> 0 us
  matrix products: 60.5 us -> 0 us
  local copies, waits for them, and re-layouts: 69.5 us -> 13.2 us
  other arithmetic: 28.9 us -> 0 us
  between operations: 14.7 us -> 0.65 us
    all_gather x4 -> x0, waiting for transfers between devices: 169 us -> none  [deliver(): result = lax.all_gather(moved, REP, axis=1, tiled=True)]
    pallas_call x0 -> x1, Pallas kernels: none -> 159 us  [shards(): pl.pallas_call(kernel, name='expert_layer', out_shape=(jax.ShapeDtypeStru...]
    all_to_all x14 -> x0, waiting for transfers between devices: 151 us -> none  [the longest x4 113 us: sum_by_axis(): lax.all_to_all(nearer.astype(jnp.bfloat16), far, split_axis=0, concat_axi...]
    all_to_all x14 -> x0, starting transfers between devices: 84.8 us -> none  [the longest x4 25.7 us: collect(): lax.all_to_all(columns, 'ep', split_axis=1, concat_axis=1, tiled=True)]
    all_to_all x6 -> x0, blocking collectives: 83 us -> none  [the longest x4 62.3 us: deliver(): lax.all_to_all(pack(rows, source_row, filled, scale), 'ep', split_axis=0,...]
    dot_general x23 -> x0, matrix products: 60.5 us -> none  [the longest x6 20.8 us: contract_first(): lax.dot_general(left, right, (((0,), (0,)), ((), ())), preferred_element_...]
    another operation x8 -> x0, local copies, waits for them, and re-layouts: 40.2 us -> none  [split_up(): array.reshape(*dims[:dim], devices, dims[dim] // devices, *dims[dim + 1:])]
    reduce_sum x22 -> x0, other arithmetic: 25.1 us -> none  [the longest x4 15.7 us: summed_on_arrival(): return arrived.astype(jnp.float32).sum(axis=0)]
  transfers between devices with their start and end apart: 18 -> 0, of which waited for: 14 -> 0; matrix products, arithmetic and copies ran while one was open for 22% -> 0% of each run, Pallas kernels for 0% -> 0%
where the time goes in v1:
time: 174 us; the launch traced here: 173 us
  Pallas kernels  159 us (91%)
  local copies, waits for them, and re-layouts  13.2 us (8%)
    pallas_call x1, Pallas kernels, shards(): pl.pallas_call(kernel, name='expert_layer', out_shape=(jax.ShapeDtypeStru...  159 us
    unnamed x13, local copies, waits for them, and re-layouts  11.9 us

profile of v1, /device:TPU:32, one launch (start us, length us, event | category | flops | bytes accessed | tf_op | source)
XLA Modules:
  0.0 172.9 jit_solution(18301174127610755951)
XLA Ops:
  0.6 1.3 pad.4.rwt
  1.9 1.5 copy.13.ids
  3.4 159.1 %expert_layer.1 = (bf16[2,128,128]{2,1,0:T(8,128)(2,1)}, bf16[2,128,128]{2,1,0:T(8,128)(2,1)}, bf16[4096,256]{1,0:T(8,128)(2,1)}, bf16[4096,256]{1,0:T(8,128)(2,...) custom-call(bf16[2,128,128]{2,1,0:T(8,128)(2,1)} %tok.1, bf16[2,128,128]{2,1,0:T(8,128)(2,1)} %cot.1, ...), custom_call_target="tpu_custom_call" | custom-call | tf_op jit(solution)/shard_map/expert_layer/pallas_call | solution.py:533
  162.5 1.5 copy.20
  163.9 1.5 copy.21
  165.4 0.0 copy-start.1
  165.4 3.2 %copy.22 = bf16[1,4096,256]{2,1,0:T(8,128)(2,1)} copy(bf16[1,4096,256]{2,1,0:T(8,128)(2,1)} %bitcast.13) | data formatting | bytes 4194304
  168.6 0.0 copy-done.1
  168.6 0.0 copy-start
  168.6 1.3 copy.23
  169.9 1.0 copy-done
  171.0 0.0 copy-start.2
  171.0 1.3 copy.24
  172.3 0.0 copy-done.2
  172.3 0.6 copy.25
Async XLA Ops:
  165.4 3.2 %copy-start.1 = (bf16[4096,256]{1,0:T(8,128)(2,1)S(1)}, bf16[4096,256]{1,0:T(8,128)(2,1)}, u32[]{:S(2)}) copy-start(bf16[4096,256]{1,0:T(8,128)(2,1)} %get-tuple-element.15) | copy-start | bytes 6291460
  168.6 2.3 %copy-start = (bf16[256,4096]{1,0:T(8,128)(2,1)S(1)}, bf16[256,4096]{1,0:T(8,128)(2,1)}, u32[]{:S(2)}) copy-start(bf16[256,4096]{1,0:T(8,128)(2,1)} %get-tuple-element.16) | copy-start | bytes 6291460
  171.0 1.3 copy-start.2

commit v2 on v1

v2 whole, which is shorter than its diff:
```python
import jax
import jax.numpy as jnp
from jax import lax
from jax.experimental import pallas as pl
from jax.experimental.pallas import tpu as pltpu
from jax.sharding import Mesh
from jax.sharding import PartitionSpec as P

MESH = pl.DeviceIdType.MESH
REP = ("zl", "x", "c")
EP = ("zh", "y")
F32 = jnp.float32
BF = jnp.bfloat16
CAP = 48
ROWS = 384
BLK = 128
HID = 256
PEERS = [(dz, dy) for dz in range(2) for dy in range(4) if dz or dy]
HALF = 192
NEAR = (0, 1, 7, 2, 6, 3, 5, 4)


def rem(value, n):
    return lax.rem(value, jnp.int32(n))


def wait(ref, sem):
    pltpu.make_async_copy(ref, ref, sem).wait()


def dot(a, b):
    return jnp.dot(a, b, preferred_element_type=F32)


def dot_tn(a, b):
    return lax.dot_general(a, b, (((0,), (0,)), ((), ())), preferred_element_type=F32)


def dot_nt(a, b):
    return lax.dot_general(a, b, (((1,), (1,)), ((), ())), preferred_element_type=F32)


def iota(rows, lanes, dim):
    return lax.broadcasted_iota(jnp.int32, (rows, lanes), dim).astype(F32)


def to_row(col):
    n = col.shape[0]
    return jnp.sum(jnp.where(iota(n, BLK, 0) == iota(n, BLK, 1), col, 0.0), axis=0, keepdims=True)


def to_col(row, n):
    return jnp.sum(jnp.where(iota(n, BLK, 0) == iota(n, BLK, 1), row, 0.0), axis=1, keepdims=True)


def tile_of(rows):
    sub = iota(8, BLK, 0)
    return jnp.where(sub == 0.0, rows[0], 0.0) + jnp.where(sub == 1.0, rows[1], 0.0)


def sigmoid(v):
    return 1.0 / (1.0 + jnp.exp(-v))


def kernel(
    tok, cot, ids, rwt, wg_h, wu_h, wd_h,
    mixed, tgrad, wg, wu, wd, rg,
    G, WgH, WuH, WdH, snd, HB, XB, AG, AU, HG, HC, PG, PU, HS, gcol, dcol,
    Pt, FX, XL, XR, zs, zr, zo, fin, ret, slots, gates, dmat, arS, arR, gts, gtr, dts, dtr, rgs, rgr,
    w_l, w_s, w_r, a_s, a_r, z_s, z_r, x_s, xl_r, xr_r, f_r, d_s, d_r, h_s, h_r,
    rx_s, rf_r, rl_r, rr_r, rz_s, rz_r, b_s, b_r, ar_s, ar_r, gt_s, gt_r, dt_s, dt_r, rg_s, rg_r, xb_s, xb_r, z3_s, z3_r,
):
    zl = lax.axis_index("zl")
    x = lax.axis_index("x")
    c = lax.axis_index("c")
    zh = lax.axis_index("zh")
    y = lax.axis_index("y")
    right, left, far = rem(x + 1, 4), rem(x + 3, 4), rem(x + 2, 4)
    z = zh * 4 + zl
    e = zh * 4 + y
    oc = 1 - c
    r = zl * 8 + x * 2 + c

    def send(src, dst, ss, rs, dev):
        pltpu.make_async_remote_copy(
            src_ref=src, dst_ref=dst, send_sem=ss, recv_sem=rs, device_id=dev, device_id_type=MESH
        ).start()

    def lanes(index, width=BLK):
        return pl.ds(pl.multiple_of(index * width, width), width)

    def feat(zl_, x_, c_):
        return zl_ * 8 + x_ * 2 + c_

    def col(arr, zl_, x_):
        return G.at[arr, :, lanes(feat(zl_, x_, c))]

    def cap(index):
        return pl.ds(pl.multiple_of(index * CAP, 16), CAP)

    mine = lanes(c, HID)

    barrier = pltpu.get_barrier_semaphore()
    pl.semaphore_signal(barrier, inc=1, device_id={"c": oc}, device_id_type=MESH)
    for j in range(1, 4):
        pl.semaphore_signal(barrier, inc=1, device_id={"x": rem(x + j, 4)}, device_id_type=MESH)
        pl.semaphore_signal(barrier, inc=1, device_id={"zl": rem(zl + j, 4)}, device_id_type=MESH)
    for j in range(1, 4):
        dev = {"zh": 1 - zh, "zl": rem(zl + j, 4)}
        pl.semaphore_signal(barrier, inc=1, device_id=dev, device_id_type=MESH)
    for dz, dy in PEERS:
        dev = {"zh": rem(zh + dz, 2), "y": rem(y + dy, 4)}
        pl.semaphore_signal(barrier, inc=1, device_id=dev, device_id_type=MESH)

    sub, lane = iota(BLK, BLK, 0), iota(BLK, BLK, 1)

    def hits(m):
        both = ids[m].astype(F32)
        first, second = to_col(both[0:1, :], BLK), to_col(both[1:2, :], BLK)
        return first, second, jnp.where(first == lane, 1.0, 0.0), jnp.where(second == lane, 1.0, 0.0)

    def route(m):
        first, second, h0, h1 = hits(m)
        tri = jnp.where(lane < sub, 1.0, 0.0).astype(BF)
        before = dot(tri, (h0 + h1).astype(BF))
        s0 = first * float(CAP) + jnp.sum(h0 * before, axis=1, keepdims=True)
        s1 = second * float(CAP) + jnp.sum(h1 * before, axis=1, keepdims=True)
        slots[m, 0] = jnp.broadcast_to(s0, (BLK, BLK))
        slots[m, 1] = jnp.broadcast_to(s1, (BLK, BLK))
        at = iota(ROWS, BLK, 0)
        match = jnp.where((at == to_row(s0)) | (at == to_row(s1)), 1.0, 0.0).astype(BF)
        for n, rows in enumerate((tok, cot)):
            arr = 2 * m + n
            snd[arr] = dot(match, rows[m]).astype(BF)
            for h in range(2):
                HB[arr, h, cap(y), :] = snd[arr, cap(h * 4 + y), :]

    def logits(m):
        _, _, h0, h1 = hits(m)
        diff = jnp.zeros((BLK, BLK), F32)
        for ex in range(8):
            diff = diff + (h0 - h1)[:, ex : ex + 1] * rwt[ex : ex + 1, :].astype(F32)
        dmat[m] = diff
        return to_row(jnp.sum(tok[m].astype(F32) * diff, axis=1, keepdims=True))

    def y_sends(m):
        for arr in (2 * m, 2 * m + 1):
            for dy in range(1, 4):
                ty = rem(y + dy, 4)
                for h in range(2):
                    send(snd.at[arr, cap(h * 4 + ty), :], HB.at[arr, h, cap(y), :],
                         a_s.at[arr], a_r.at[arr], {"y": ty})

    route(0)
    pl.semaphore_wait(barrier, 17)

    def ar_one(k):
        for j in range(1, 4):
            send(arS.at[k, 0], arR.at[k, j - 1], ar_s.at[k, 0], ar_r.at[k, j - 1], {"zl": rem(zl + j, 4)})

    def ar_two(k):
        total = arS[k, 0]
        for j in range(3):
            wait(arR.at[k, j], ar_r.at[k, j])
            total = total + arR[k, j]
        arS[k, 1] = total
        for j in range(1, 4):
            send(arS.at[k, 1], arR.at[k, 2 + j], ar_s.at[k, 1], ar_r.at[k, 2 + j], {"x": rem(x + j, 4)})

    def ar_three(k):
        total = arS[k, 1]
        for j in range(3, 6):
            wait(arR.at[k, j], ar_r.at[k, j])
            total = total + arR[k, j]
        arS[k, 2] = total
        send(arS.at[k, 2], arR.at[k, 6], ar_s.at[k, 2], ar_r.at[k, 6], {"c": oc})

    def ar_end(k):
        wait(arR.at[k, 6], ar_r.at[k, 6])
        return arS[k, 2] + arR[k, 6]


    y_sends(0)
    arS[0, 0] = tile_of([logits(0), logits(1)])
    ar_one(0)
    route(1)
    y_sends(1)

    pltpu.make_async_copy(wg_h, wg, w_l.at[0]).start()
    pltpu.make_async_copy(wu_h, wu, w_l.at[1]).start()
    pltpu.make_async_copy(wd_h, wd, w_l.at[2]).start()

    @pl.loop(0, 16)
    def _(b):
        at = feat(b // 4, b % 4, c)
        pltpu.make_async_copy(wg_h.at[lanes(at), :], WgH.at[lanes(b), mine], w_l.at[3]).start()
        pltpu.make_async_copy(wu_h.at[lanes(at), :], WuH.at[lanes(b), mine], w_l.at[4]).start()
        pltpu.make_async_copy(wd_h.at[:, lanes(at)], WdH.at[mine, lanes(b)], w_l.at[5]).start()

    @pl.loop(0, 16)
    def _(b):
        at = feat(b // 4, b % 4, oc)
        send(wg_h.at[lanes(at), :], WgH.at[lanes(b), mine], w_s.at[0], w_r.at[0], {"c": oc})
        send(wu_h.at[lanes(at), :], WuH.at[lanes(b), mine], w_s.at[1], w_r.at[1], {"c": oc})
        send(wd_h.at[:, lanes(at)], WdH.at[mine, lanes(b)], w_s.at[2], w_r.at[2], {"c": oc})

    def place(arr, z8, x_):
        return G.at[arr, pl.ds(pl.multiple_of(z8 // 4 * HALF, HALF), HALF), lanes(feat(rem(z8, 4), x_, c))]

    def spread_block(arr, z8, j):
        here = place(arr, z8, x)
        send(here, here, x_s.at[arr], xl_r.at[arr, j], {"x": right})
        send(here, here, x_s.at[arr], xr_r.at[arr, j], {"x": left})
        send(here, here, d_s.at[arr], d_r.at[arr], {"c": oc})

    def at_z(z8):
        return {"zh": z8 // 4, "zl": rem(z8, 4)}

    def stage_a(arr):
        wait(snd.at[arr, 0:288, :], a_r.at[arr])
        here = place(arr, z, x)
        for j in range(1, 8):
            to = rem(z + 8 - NEAR[j], 8)
            send(HB.at[arr, to // 4], here, z_s.at[arr], z_r.at[arr, j], at_z(to))
        here[...] = HB[arr, zh]
        spread_block(arr, z, 0)

    def stage_b(arr):
        for j in range(1, 8):
            zj = rem(z + NEAR[j], 8)
            wait(place(arr, zj, x), z_r.at[arr, j])
            spread_block(arr, zj, j)

    def stage_c(arr):
        for j in range(8):
            zj = rem(z + NEAR[j], 8)
            here = place(arr, zj, left)
            wait(here, xl_r.at[arr, j])
            if j % 2 == 0:
                send(here, here, x_s.at[arr], f_r.at[arr, j], {"x": right})
            send(here, here, d_s.at[arr], d_r.at[arr], {"c": oc})
            here = place(arr, zj, right)
            wait(here, xr_r.at[arr, j])
            if j % 2 == 1:
                send(here, here, x_s.at[arr], f_r.at[arr, j], {"x": left})
            send(here, here, d_s.at[arr], d_r.at[arr], {"c": oc})

    def b_start():
        wait(snd.at[3, 0:288, :], a_r.at[3])
        send(HB.at[3], XB.at[0], xb_s.at[0], xb_r.at[0], {"x": right})
        send(HB.at[3], XB.at[1], xb_s.at[0], xb_r.at[1], {"x": left})

    def b_forward():
        wait(XB.at[0], xb_r.at[0])
        send(XB.at[0, 0], XB.at[2, 0], xb_s.at[0], xb_r.at[2], {"x": right})
        wait(XB.at[1], xb_r.at[1])
        send(XB.at[1, 1], XB.at[2, 1], xb_s.at[0], xb_r.at[3], {"x": left})

    def b_out(q, src, x_):
        here = place(3, z, x_)
        for j in range(1, 8):
            to = rem(z + 8 - NEAR[j], 8)
            send(src.at[to // 4], here, z3_s.at[0], z3_r.at[q, j], at_z(to))
        here[...] = src[zh]
        send(here, here, d_s.at[3], d_r.at[3], {"c": oc})

    def b_spread():
        b_out(0, HB.at[3], x)
        b_out(1, XB.at[0], left)
        b_out(2, XB.at[1], right)
        wait(XB.at[2, 0], xb_r.at[2])
        wait(XB.at[2, 1], xb_r.at[3])
        b_out(3, XB.at[2], far)

    def b_take(q):
        for j in range(1, 8):
            here = place(3, rem(z + NEAR[j], 8), (x, left, right, far)[q])
            wait(here, z3_r.at[q, j])
            send(here, here, d_s.at[3], d_r.at[3], {"c": oc})

    def stage_d(arr):
        for j in range(8):
            here = place(arr, rem(z + NEAR[j], 8), far)
            wait(here, f_r.at[arr, j])
            send(here, here, d_s.at[arr], d_r.at[arr], {"c": oc})

    def stage_e(arr):
        wait(G.at[arr, :, 0:2048], d_r.at[arr])

    def make_gates():
        total = ar_end(0)
        for m in range(2):
            diff = to_col(total[m : m + 1, :], BLK)
            gates[m, 0] = jnp.broadcast_to(sigmoid(diff), (BLK, BLK))
            gates[m, 1] = jnp.broadcast_to(sigmoid(-diff), (BLK, BLK))

        @pl.loop(0, 8)
        def _(ex):
            at = lane + (ex * CAP).astype(F32)
            rows = []
            for m in range(2):
                picked = jnp.where(slots[m, 0] == at, gates[m, 0], 0.0)
                picked = picked + jnp.where(slots[m, 1] == at, gates[m, 1], 0.0)
                rows.append(jnp.sum(picked, axis=0, keepdims=True))
            gts[ex] = tile_of(rows)

        gtr[e] = gts[e]
        for n, (dz, dy) in enumerate(PEERS):
            tz, ty = rem(zh + dz, 2), rem(y + dy, 4)
            send(gts.at[tz * 4 + ty], gtr.at[e], gt_s.at[0], gt_r.at[0], {"zh": tz, "y": ty})

    def take_gates():
        wait(gts.at[0:7], gt_r.at[0])

        @pl.loop(0, 8)
        def _(s):
            tile = gtr[s]
            for m in range(2):
                gcol[m, cap(s), :] = jnp.broadcast_to(to_col(tile[m : m + 1, :], CAP), (CAP, BLK))

    def pre(m):
        AG[...] = jnp.zeros_like(AG)
        AU[...] = jnp.zeros_like(AU)

        @pl.loop(0, 4)
        def _(k):
            rows = G[2 * m, :, lanes(k, 1024)]
            AG[...] += dot(rows, wg[lanes(k, 1024), :])
            AU[...] += dot(rows, wu[lanes(k, 1024), :])

    def back(m):
        HG[...] = jnp.zeros_like(HG)

        @pl.loop(0, 4)
        def _(k):
            HG[...] += dot_nt(G[2 * m + 1, :, lanes(k, 1024)], wd[:, lanes(k, 1024)])

        @pl.loop(0, 6)
        def _(i):
            rows = lanes(i, 64)
            pg, pu, hr = AG[rows, :], AU[rows, :], HG[rows, :]
            g = gcol[m, rows, 0:1]
            sig = sigmoid(pg)
            act = pg * sig
            hb = (act * pu).astype(BF)
            hw = hb.astype(F32)
            dcol[m, rows, :] = jnp.broadcast_to(jnp.sum(hw * hr, axis=1, keepdims=True), (64, BLK))
            hs = hr * g
            HC[m, rows, mine] = hb
            PG[m, rows, mine] = (hs * pu * (sig * (1.0 + pg * (1.0 - sig)))).astype(BF)
            PU[m, rows, mine] = (hs * act).astype(BF)
            HS[m, rows, :] = (hw * g).astype(BF)

        for n, buf in enumerate((HC, PG, PU)):
            send(buf.at[m, :, mine], buf.at[m, :, mine], h_s.at[m, n], h_r.at[m, n], {"c": oc})

    def part(a, zl_, x_):
        return Pt.at[a, :, lanes(zl_ * 4 + x_)]

    def far_sends(a):
        for zp in range(4):
            to = right if zp % 2 == 0 else left
            send(part(a, zp, far), FX.at[a, zp], rx_s.at[a], rf_r.at[a, zp], {"x": to})

    def near_sends(a):
        for zp in range(4):
            if zp % 2 == 0:
                send(part(a, zp, left), XR.at[a, zp], rx_s.at[a], rr_r.at[a, zp], {"x": left})
            else:
                send(part(a, zp, right), XL.at[a, zp], rx_s.at[a], rl_r.at[a, zp], {"x": right})

    def outs(m):
        wait(HC.at[m, :, 0:HID], h_r.at[m, 0])

        @pl.loop(0, 4)
        def _(q):
            Pt[2 * m, :, lanes(q, 512)] = dot(HC[m], WdH[:, lanes(q, 512)]).astype(BF)

    def ins(m):
        wait(PG.at[m, :, 0:HID], h_r.at[m, 1])
        wait(PU.at[m, :, 0:HID], h_r.at[m, 2])

        @pl.loop(0, 4)
        def _(q):
            at = lanes(q, 512)
            Pt[2 * m + 1, :, at] = (dot_nt(PG[m], WgH[at, :]) + dot_nt(PU[m], WuH[at, :])).astype(BF)

    def second_sends(a):
        for zp in range(4):
            wait(FX.at[a, zp], rf_r.at[a, zp])
            tx = right if zp % 2 == 0 else left
            where = lanes(zp * 4 + tx)
            Pt[a, :, where] = (Pt[a, :, where].astype(F32) + FX[a, zp].astype(F32)).astype(BF)
            if zp % 2 == 0:
                send(part(a, zp, tx), XL.at[a, zp], rx_s.at[a], rl_r.at[a, zp], {"x": right})
            else:
                send(part(a, zp, tx), XR.at[a, zp], rx_s.at[a], rr_r.at[a, zp], {"x": left})

    def third_sends(a, zps=(0, 1, 2, 3)):
        for zp in zps:
            wait(XL.at[a, zp], rl_r.at[a, zp])
            wait(XR.at[a, zp], rr_r.at[a, zp])
            total = Pt[a, :, lanes(zp * 4 + x)].astype(F32)
            total = total + XL[a, zp].astype(F32) + XR[a, zp].astype(F32)
            for h in range(2):
                to = h * 4 + zp
                step = rem(z + 8 - to, 8)
                rows = total[h * HALF : (h + 1) * HALF, :]
                zs[a, to] = rows.astype(BF)

                @pl.when(z == to)
                def _():
                    zo[a, zh] = rows
                    zo[a, 1 - zh] = jnp.zeros((HALF, BLK), F32)

                @pl.when(z != to)
                def _():
                    send(zs.at[a, to], zr.at[a, step - 1], rz_s.at[a], rz_r.at[a, step - 1], {"zh": h, "zl": zp})

    def finish(a):
        for j in range(1, 8):
            step = NEAR[j]
            h = rem(z + step, 8) // 4
            wait(zr.at[a, step - 1], rz_r.at[a, step - 1])
            zo[a, h] += zr[a, step - 1].astype(F32)
        for h in range(2):
            fin[a, h] = zo[a, h].astype(BF)
            ret[a, cap(h * 4 + y), :] = fin[a, h, cap(y), :]
        for dy in range(1, 4):
            ty = rem(y + dy, 4)
            for h in range(2):
                send(fin.at[a, h, cap(ty), :], ret.at[a, cap(h * 4 + y), :], b_s.at[a], b_r.at[a], {"y": ty})

    def send_dots():
        @pl.loop(0, 8)
        def _(s):
            dts[s] = tile_of([to_row(dcol[m, cap(s), :]) for m in range(2)])

        dtr[e] = dts[e]
        for dz, dy in PEERS:
            tz, ty = rem(zh + dz, 2), rem(y + dy, 4)
            send(dts.at[tz * 4 + ty], dtr.at[e], dt_s.at[0], dt_r.at[0], {"zh": tz, "y": ty})

    def take_dots():
        wait(dts.at[0:7], dt_r.at[0])
        rows = []
        for m in range(2):
            total = jnp.zeros((BLK, BLK), F32)
            for ex in range(8):
                at = lane + float(ex * CAP)
                row = dtr[ex][m : m + 1, :]
                total = total + jnp.where(slots[m, 0] == at, row, 0.0) - jnp.where(slots[m, 1] == at, row, 0.0)
            rows.append(to_row(jnp.sum(total, axis=1, keepdims=True)))
        arS[1, 0] = tile_of(rows)
        ar_one(1)

    def weight_grads(lo, hi):
        @pl.loop(lo, hi)
        def _(i):
            at = lanes(i, 512)
            t0, t1 = G[0, :, at], G[2, :, at]
            wg[at, :] = (dot_tn(t0, PG[0, :, mine]) + dot_tn(t1, PG[1, :, mine])).astype(BF)
            wu[at, :] = (dot_tn(t0, PU[0, :, mine]) + dot_tn(t1, PU[1, :, mine])).astype(BF)
            wd[:, at] = (dot_tn(HS[0], G[1, :, at]) + dot_tn(HS[1], G[3, :, at])).astype(BF)

    stage_a(0)
    stage_a(1)
    b_start()
    stage_a(2)
    ar_two(0)
    b_forward()
    ar_three(0)
    make_gates()
    b_spread()
    stage_b(0)
    stage_c(0)
    stage_b(1)
    stage_d(0)
    stage_c(1)
    stage_b(2)
    stage_e(0)
    for k, buf in enumerate((wg, wu, wd)):
        pltpu.make_async_copy(buf, buf, w_l.at[k]).wait()
    for k, half in enumerate((WgH.at[:, 0:HID], WuH.at[:, 0:HID], WdH.at[0:HID, :])):
        wait(half, w_l.at[3 + k])
        wait(half, w_r.at[k])
    pre(0)
    stage_d(1)
    stage_c(2)
    stage_e(1)
    take_gates()
    back(0)
    outs(0)
    far_sends(0)
    near_sends(0)
    ins(0)
    stage_d(2)
    far_sends(1)
    second_sends(0)
    near_sends(1)
    b_take(0)
    stage_e(2)
    pre(1)
    b_take(1)
    second_sends(1)
    b_take(2)
    b_take(3)
    stage_e(3)
    back(1)
    outs(1)
    far_sends(2)
    near_sends(2)
    send_dots()
    ins(1)
    far_sends(3)
    second_sends(2)
    near_sends(3)
    third_sends(0)
    third_sends(1)
    weight_grads(0, 3)
    take_dots()
    third_sends(2, (0, 1))
    second_sends(3)
    third_sends(2, (2, 3))
    weight_grads(3, 5)
    finish(0)
    ar_two(1)
    finish(1)
    third_sends(3, (0, 1))
    weight_grads(5, 7)
    ar_three(1)
    third_sends(3, (2, 3))
    weight_grads(7, 8)

    total = ar_end(1)
    share = jnp.zeros((BLK, BLK), F32)
    deltas = []
    for m in range(2):
        _, _, h0, h1 = hits(m)
        delta = to_col(total[m : m + 1, :], BLK) * gates[m, 0] * gates[m, 1]
        deltas.append(delta)
        share = share + lax.dot_general(
            delta * (h0 - h1), tok[m].astype(F32), (((0,), (0,)), ((), ())),
            preferred_element_type=F32, precision=lax.Precision.HIGHEST,
        )
    rgs[...] = share[0:8, :]
    for n, (dz, dy) in enumerate(PEERS):
        tz, ty = rem(zh + dz, 2), rem(y + dy, 4)
        send(rgs, rgr.at[n], rg_s.at[0], rg_r.at[n], {"zh": tz, "y": ty})
    finish(2)
    finish(3)

    for m in range(2):
        a = 2 * m
        wait(ret.at[a, 0:288, :], b_r.at[a])
        wait(ret.at[a + 1, 0:288, :], b_r.at[a + 1])
        one = jnp.zeros((BLK, BLK), F32)
        two = jnp.zeros((BLK, BLK), F32)
        grad = deltas[m] * dmat[m]
        for q in range(3):
            at = lane + float(q * BLK)
            p0 = jnp.where(slots[m, 0] == at, 1.0, 0.0)
            p1 = jnp.where(slots[m, 1] == at, 1.0, 0.0)
            rows = ret[a, q * BLK : (q + 1) * BLK, :]
            one = one + dot(p0.astype(BF), rows)
            two = two + dot(p1.astype(BF), rows)
            grad = grad + dot((p0 + p1).astype(BF), ret[a + 1, q * BLK : (q + 1) * BLK, :])
        mixed[m] = (gates[m, 0] * one + gates[m, 1] * two).astype(BF)
        tgrad[m] = grad.astype(BF)

    whole = rgs[...]
    for n in range(7):
        wait(rgr.at[n], rg_r.at[n])
        whole = whole + rgr[n]
    rg[...] = whole

    for arr in range(4):
        wait(snd.at[arr, 0:288, :], a_s.at[arr])
        if arr < 3:
            wait(G.at[arr, 0:HALF, 0:896], z_s.at[arr])
            wait(G.at[arr, :, 0:1536], x_s.at[arr])
        wait(G.at[arr, :, 0:2048], d_s.at[arr])
        wait(Pt.at[arr, :, 0:1536], rx_s.at[arr])
        wait(zr.at[arr], rz_s.at[arr])
        wait(ret.at[arr, 0:288, :], b_s.at[arr])
    wait(zr.at[0, 0:6], xb_s.at[0])
    wait(G.at[3, 0:HALF, 0:3584], z3_s.at[0])
    for k, half in enumerate((WgH.at[:, 0:HID], WuH.at[:, 0:HID], WdH.at[0:HID, :])):
        wait(half, w_s.at[k])
    for m in range(2):
        for n, buf in enumerate((HC, PG, PU)):
            wait(buf.at[m, :, 0:HID], h_s.at[m, n])
    for k in range(2):
        wait(arR.at[k, 0:3], ar_s.at[k, 0])
        wait(arR.at[k, 3:6], ar_s.at[k, 1])
        wait(arR.at[k, 6], ar_s.at[k, 2])
    wait(gts.at[0:7], gt_s.at[0])
    wait(dts.at[0:7], dt_s.at[0])
    wait(rgr.at[0:7], rg_s.at[0])


def write_out(*refs):
    sems = refs[12]
    copies = [pltpu.make_async_copy(refs[k], refs[6 + k], sems.at[k]) for k in range(6)]
    for copy in copies:
        copy.start()
    for copy in copies:
        copy.wait()


def shards(tokens, expert_ids, router_weight, w_gate, w_up, w_down, cotangent):
    big = lambda *dims: pltpu.VMEM(dims, BF)
    wide = lambda *dims: pltpu.VMEM(dims, F32)
    dma = lambda *dims: pltpu.SemaphoreType.DMA(dims)
    vm = pl.BlockSpec(memory_space=pltpu.VMEM)
    anyw = pl.BlockSpec(memory_space=pl.ANY)
    D = 4096
    results = pl.pallas_call(
        kernel,
        name="expert_layer",
        out_shape=(
            big(2, BLK, BLK), big(2, BLK, BLK), big(D, HID), big(D, HID), big(HID, D), wide(8, BLK),
        ),
        in_specs=[vm, vm, vm, vm, anyw, anyw, anyw],
        out_specs=(vm,) * 6,
        scratch_shapes=[
            big(4, ROWS, D),
            big(2048, 512), big(2048, 512), big(512, 2048), big(4, ROWS, BLK), big(4, 2, HALF, BLK), big(3, 2, HALF, BLK),
            wide(ROWS, HID), wide(ROWS, HID), wide(ROWS, HID),
            big(2, ROWS, 512), big(2, ROWS, 512), big(2, ROWS, 512), big(2, ROWS, HID),
            wide(2, ROWS, BLK), wide(2, ROWS, BLK),
            big(4, ROWS, 2048), big(4, 4, ROWS, BLK), big(4, 4, ROWS, BLK), big(4, 4, ROWS, BLK),
            big(4, 8, HALF, BLK), big(4, 7, HALF, BLK), wide(4, 2, HALF, BLK), big(4, 2, HALF, BLK), big(4, ROWS, BLK),
            wide(2, 2, BLK, BLK), wide(2, 2, BLK, BLK), wide(2, BLK, BLK),
            wide(2, 3, 8, BLK), wide(2, 7, 8, BLK), wide(8, 8, BLK), wide(8, 8, BLK), wide(8, 8, BLK), wide(8, 8, BLK),
            wide(8, BLK), wide(7, 8, BLK),
            dma(6), dma(3), dma(3), dma(4), dma(4), dma(4), dma(3, 8), dma(4), dma(3, 8), dma(3, 8), dma(3, 8),
            dma(4), dma(4), dma(2, 3), dma(2, 3),
            dma(4), dma(4, 4), dma(4, 4), dma(4, 4), dma(4), dma(4, 7), dma(4), dma(4),
            dma(2, 3), dma(2, 7), dma(1), dma(1), dma(1), dma(1), dma(1), dma(7), dma(1), dma(4), dma(1), dma(4, 8),
        ],
        compiler_params=pltpu.CompilerParams(
            collective_id=0, has_side_effects=True, vmem_limit_bytes=52 * 1024 * 1024
        ),
    )(tokens, cotangent, expert_ids.transpose(0, 2, 1), router_weight.T, w_gate[0], w_up[0], w_down[0])
    mixed, tgrad, gg, ug, dg, rg = pl.pallas_call(
        write_out,
        name="write_out",
        out_shape=tuple(jax.ShapeDtypeStruct(v.shape, v.dtype) for v in results),
        in_specs=[vm] * 6,
        out_specs=(anyw,) * 6,
        scratch_shapes=[dma(6)],
        compiler_params=pltpu.CompilerParams(vmem_limit_bytes=1024 * 1024),
    )(*(pltpu.with_memory_space_constraint(v, pltpu.VMEM) for v in results))
    return mixed, tgrad, gg[None], ug[None], dg[None], rg.T


def solution(mesh):
    split = Mesh(mesh.devices.reshape(4, 4, 2, 2, 4), REP + EP)
    in_specs = (
        P(None, EP, REP),
        P(None, EP, None),
        P(REP, None),
        P(EP, None, REP),
        P(EP, None, REP),
        P(EP, REP, None),
        P(None, EP, REP),
    )
    out_specs = (
        P(None, EP, REP),
        P(None, EP, REP),
        P(EP, None, REP),
        P(EP, None, REP),
        P(EP, REP, None),
        P(REP, None),
    )
    return jax.shard_map(shards, mesh=split, in_specs=in_specs, out_specs=out_specs, check_vma=False)
```

time: 174 us -> 143 us (0.82)
  Pallas kernels: 159 us -> 140 us
  local copies, waits for them, and re-layouts: 13.2 us -> 0 us
    pallas_call x1 -> x2, Pallas kernels: 159 us -> 140 us  [the longest x1 138 us: shards(): pl.pallas_call(kernel, name='expert_layer', out_shape=(big(2, BLK, BLK),...]
    unnamed x13 -> x0, local copies, waits for them, and re-layouts: 11.9 us -> none
where the time goes in v2:
time: 143 us; the launch traced here: 141 us
  Pallas kernels  140 us (98%)
    pallas_call x1, Pallas kernels, shards(): pl.pallas_call(kernel, name='expert_layer', out_shape=(big(2, BLK, BLK),...  138 us

profile of v2, /device:TPU:32, one launch (start us, length us, event | category | flops | bytes accessed | tf_op | source)
XLA Modules:
  0.0 141.3 jit_solution(18316448122820084681)
XLA Ops:
  0.6 137.7 %expert_layer.1 = (bf16[2,128,128]{2,1,0:T(8,128)(2,1)S(1)}, bf16[2,128,128]{2,1,0:T(8,128)(2,1)S(1)}, bf16[4096,256]{1,0:T(8,128)(2,1)S(1)}, bf16[4096,256]{1,0...) custom-call(bf16[2,128,128]{2,1,0:T(8,128)(2,1)} %tok.1, bf16[2,128,128]{2,1,0:T(8,128)(2,1)} %cot.1, ...), custom_call_target="tpu_custom_call" | custom-call | tf_op jit(solution)/shard_map/expert_layer/pallas_call | solution.py:618
  138.3 2.8 %write_out.1 = (bf16[2,128,128]{2,1,0:T(8,128)(2,1)}, bf16[2,128,128]{2,1,0:T(8,128)(2,1)}, bf16[4096,256]{1,0:T(8,128)(2,1)}, bf16[4096,256]{1,0:T(8,128)(2,1)}...) custom-call(bf16[2,128,128]{2,1,0:T(8,128)(2,1)S(1)} %get-tuple-element.18.refs_0_, ...), custom_call_target="tpu_custom_call" | custom-call | tf_op jit(solution)/shard_map/write_out/pallas_call | solution.py:646

commit v3 on v2

--- a/solution.py
+++ b/solution.py
@@ -17,6 +17,7 @@
 HID = 256
 PEERS = [(dz, dy) for dz in range(2) for dy in range(4) if dz or dy]
 HALF = 192
+TURN = (0, 1, 3, 2)
 NEAR = (0, 1, 7, 2, 6, 3, 5, 4)
 
 
@@ -149,34 +150,34 @@
                 ty = rem(y + dy, 4)
                 for h in range(2):
                     send(snd.at[arr, cap(h * 4 + ty), :], HB.at[arr, h, cap(y), :],
-                         a_s.at[arr], a_r.at[arr], {"y": ty})
+                         a_s.at[0], a_r.at[arr], {"y": ty})
 
     route(0)
     pl.semaphore_wait(barrier, 17)
 
     def ar_one(k):
         for j in range(1, 4):
-            send(arS.at[k, 0], arR.at[k, j - 1], ar_s.at[k, 0], ar_r.at[k, j - 1], {"zl": rem(zl + j, 4)})
+            send(arS.at[k, 0], arR.at[k, j - 1], ar_s.at[0], ar_r.at[k, 0], {"zl": rem(zl + j, 4)})
 
     def ar_two(k):
         total = arS[k, 0]
+        wait(arR.at[k, 0:3], ar_r.at[k, 0])
         for j in range(3):
-            wait(arR.at[k, j], ar_r.at[k, j])
             total = total + arR[k, j]
         arS[k, 1] = total
         for j in range(1, 4):
-            send(arS.at[k, 1], arR.at[k, 2 + j], ar_s.at[k, 1], ar_r.at[k, 2 + j], {"x": rem(x + j, 4)})
+            send(arS.at[k, 1], arR.at[k, 2 + j], ar_s.at[0], ar_r.at[k, 1], {"x": rem(x + j, 4)})
 
     def ar_three(k):
         total = arS[k, 1]
+        wait(arR.at[k, 3:6], ar_r.at[k, 1])
         for j in range(3, 6):
-            wait(arR.at[k, j], ar_r.at[k, j])
             total = total + arR[k, j]
         arS[k, 2] = total
-        send(arS.at[k, 2], arR.at[k, 6], ar_s.at[k, 2], ar_r.at[k, 6], {"c": oc})
+        send(arS.at[k, 2], arR.at[k, 6], ar_s.at[0], ar_r.at[k, 2], {"c": oc})
 
     def ar_end(k):
-        wait(arR.at[k, 6], ar_r.at[k, 6])
+        wait(arR.at[k, 6], ar_r.at[k, 2])
         return arS[k, 2] + arR[k, 6]
 
 
@@ -209,9 +210,9 @@
 
     def spread_block(arr, z8, j):
         here = place(arr, z8, x)
-        send(here, here, x_s.at[arr], xl_r.at[arr, j], {"x": right})
-        send(here, here, x_s.at[arr], xr_r.at[arr, j], {"x": left})
-        send(here, here, d_s.at[arr], d_r.at[arr], {"c": oc})
+        send(here, here, x_s.at[0], xl_r.at[arr, j], {"x": right})
+        send(here, here, x_s.at[0], xr_r.at[arr, j], {"x": left})
+        send(here, here, d_s.at[0], d_r.at[arr], {"c": oc})
 
     def at_z(z8):
         return {"zh": z8 // 4, "zl": rem(z8, 4)}
@@ -221,7 +222,7 @@
         here = place(arr, z, x)
         for j in range(1, 8):
             to = rem(z + 8 - NEAR[j], 8)
-            send(HB.at[arr, to // 4], here, z_s.at[arr], z_r.at[arr, j], at_z(to))
+            send(HB.at[arr, to // 4], here, z_s.at[0], z_r.at[arr, j], at_z(to))
         here[...] = HB[arr, zh]
         spread_block(arr, z, 0)
 
@@ -237,13 +238,13 @@
             here = place(arr, zj, left)
             wait(here, xl_r.at[arr, j])
             if j % 2 == 0:
-                send(here, here, x_s.at[arr], f_r.at[arr, j], {"x": right})
-            send(here, here, d_s.at[arr], d_r.at[arr], {"c": oc})
+                send(here, here, x_s.at[0], f_r.at[arr, j], {"x": right})
+            send(here, here, d_s.at[0], d_r.at[arr], {"c": oc})
             here = place(arr, zj, right)
             wait(here, xr_r.at[arr, j])
             if j % 2 == 1:
-                send(here, here, x_s.at[arr], f_r.at[arr, j], {"x": left})
-            send(here, here, d_s.at[arr], d_r.at[arr], {"c": oc})
+                send(here, here, x_s.at[0], f_r.at[arr, j], {"x": left})
+            send(here, here, d_s.at[0], d_r.at[arr], {"c": oc})
 
     def b_start():
         wait(snd.at[3, 0:288, :], a_r.at[3])
@@ -260,9 +261,9 @@
         here = place(3, z, x_)
         for j in range(1, 8):
             to = rem(z + 8 - NEAR[j], 8)
-            send(src.at[to // 4], here, z3_s.at[0], z3_r.at[q, j], at_z(to))
+            send(src.at[to // 4], here, z3_s.at[0], z3_r.at[q], at_z(to))
         here[...] = src[zh]
-        send(here, here, d_s.at[3], d_r.at[3], {"c": oc})
+        send(here, here, d_s.at[0], d_r.at[3], {"c": oc})
 
     def b_spread():
         b_out(0, HB.at[3], x)
@@ -273,16 +274,16 @@
         b_out(3, XB.at[2], far)
 
     def b_take(q):
+        wait(zr.at[0], z3_r.at[q])
         for j in range(1, 8):
             here = place(3, rem(z + NEAR[j], 8), (x, left, right, far)[q])
-            wait(here, z3_r.at[q, j])
-            send(here, here, d_s.at[3], d_r.at[3], {"c": oc})
+            send(here, here, d_s.at[0], d_r.at[3], {"c": oc})
 
     def stage_d(arr):
         for j in range(8):
             here = place(arr, rem(z + NEAR[j], 8), far)
             wait(here, f_r.at[arr, j])
-            send(here, here, d_s.at[arr], d_r.at[arr], {"c": oc})
+            send(here, here, d_s.at[0], d_r.at[arr], {"c": oc})
 
     def stage_e(arr):
         wait(G.at[arr, :, 0:2048], d_r.at[arr])
@@ -328,6 +329,15 @@
             AG[...] += dot(rows, wg[lanes(k, 1024), :])
             AU[...] += dot(rows, wu[lanes(k, 1024), :])
 
+    def hid(m):
+        @pl.loop(0, 6)
+        def _(i):
+            rows = lanes(i, 64)
+            pg = AG[rows, :]
+            HC[m, rows, mine] = (pg * sigmoid(pg) * AU[rows, :]).astype(BF)
+
+        send(HC.at[m, :, mine], HC.at[m, :, mine], h_s.at[0], h_r.at[m, 0], {"c": oc})
+
     def back(m):
         HG[...] = jnp.zeros_like(HG)
 
@@ -342,32 +352,30 @@
             g = gcol[m, rows, 0:1]
             sig = sigmoid(pg)
             act = pg * sig
-            hb = (act * pu).astype(BF)
-            hw = hb.astype(F32)
+            hw = HC[m, rows, mine].astype(F32)
             dcol[m, rows, :] = jnp.broadcast_to(jnp.sum(hw * hr, axis=1, keepdims=True), (64, BLK))
             hs = hr * g
-            HC[m, rows, mine] = hb
             PG[m, rows, mine] = (hs * pu * (sig * (1.0 + pg * (1.0 - sig)))).astype(BF)
             PU[m, rows, mine] = (hs * act).astype(BF)
             HS[m, rows, :] = (hw * g).astype(BF)
 
-        for n, buf in enumerate((HC, PG, PU)):
-            send(buf.at[m, :, mine], buf.at[m, :, mine], h_s.at[m, n], h_r.at[m, n], {"c": oc})
-
-    def part(a, zl_, x_):
-        return Pt.at[a, :, lanes(zl_ * 4 + x_)]
+        for n, buf in enumerate((PG, PU)):
+            send(buf.at[m, :, mine], buf.at[m, :, mine], h_s.at[0], h_r.at[m, 1 + n], {"c": oc})
+
+    def spot(p, x_):
+        return lanes(rem(zl + TURN[p], 4) * 4 + x_)
 
     def far_sends(a):
-        for zp in range(4):
-            to = right if zp % 2 == 0 else left
-            send(part(a, zp, far), FX.at[a, zp], rx_s.at[a], rf_r.at[a, zp], {"x": to})
-
-    def near_sends(a):
-        for zp in range(4):
-            if zp % 2 == 0:
-                send(part(a, zp, left), XR.at[a, zp], rx_s.at[a], rr_r.at[a, zp], {"x": left})
+        for p in range(4):
+            to = right if p % 2 == 0 else left
+            send(Pt.at[a, :, spot(p, far)], FX.at[a, p], rx_s.at[0], rf_r.at[a, p], {"x": to})
+
+    def near_sends(a, ps=(0, 1, 2, 3)):
+        for p in ps:
+            if p % 2 == 0:
+                send(Pt.at[a, :, spot(p, left)], XR.at[a, p], rx_s.at[0], rr_r.at[a, p], {"x": left})
             else:
-                send(part(a, zp, right), XL.at[a, zp], rx_s.at[a], rl_r.at[a, zp], {"x": right})
+                send(Pt.at[a, :, spot(p, right)], XL.at[a, p], rx_s.at[0], rl_r.at[a, p], {"x": right})
 
     def outs(m):
         wait(HC.at[m, :, 0:HID], h_r.at[m, 0])
@@ -385,51 +393,54 @@
             at = lanes(q, 512)
             Pt[2 * m + 1, :, at] = (dot_nt(PG[m], WgH[at, :]) + dot_nt(PU[m], WuH[at, :])).astype(BF)
 
-    def second_sends(a):
-        for zp in range(4):
-            wait(FX.at[a, zp], rf_r.at[a, zp])
-            tx = right if zp % 2 == 0 else left
-            where = lanes(zp * 4 + tx)
-            Pt[a, :, where] = (Pt[a, :, where].astype(F32) + FX[a, zp].astype(F32)).astype(BF)
-            if zp % 2 == 0:
-                send(part(a, zp, tx), XL.at[a, zp], rx_s.at[a], rl_r.at[a, zp], {"x": right})
+    def second_sends(a, ps=(0, 1, 2, 3)):
+        for p in ps:
+            wait(FX.at[a, p], rf_r.at[a, p])
+            tx = right if p % 2 == 0 else left
+            here = spot(p, tx)
+            Pt[a, :, here] = (Pt[a, :, here].astype(F32) + FX[a, p].astype(F32)).astype(BF)
+            if p % 2 == 0:
+                send(Pt.at[a, :, here], XL.at[a, p], rx_s.at[0], rl_r.at[a, p], {"x": right})
             else:
-                send(part(a, zp, tx), XR.at[a, zp], rx_s.at[a], rr_r.at[a, zp], {"x": left})
-
-    def third_sends(a, zps=(0, 1, 2, 3)):
-        for zp in zps:
-            wait(XL.at[a, zp], rl_r.at[a, zp])
-            wait(XR.at[a, zp], rr_r.at[a, zp])
-            total = Pt[a, :, lanes(zp * 4 + x)].astype(F32)
-            total = total + XL[a, zp].astype(F32) + XR[a, zp].astype(F32)
+                send(Pt.at[a, :, here], XR.at[a, p], rx_s.at[0], rr_r.at[a, p], {"x": left})
+
+    def third_sends(a, ps=(0, 1, 2, 3)):
+        for p in ps:
+            wait(XL.at[a, p], rl_r.at[a, p])
+            wait(XR.at[a, p], rr_r.at[a, p])
+            total = Pt[a, :, spot(p, x)].astype(F32)
+            total = total + XL[a, p].astype(F32) + XR[a, p].astype(F32)
+            zp = rem(zl + TURN[p], 4)
             for h in range(2):
                 to = h * 4 + zp
-                step = rem(z + 8 - to, 8)
                 rows = total[h * HALF : (h + 1) * HALF, :]
-                zs[a, to] = rows.astype(BF)
-
-                @pl.when(z == to)
-                def _():
-                    zo[a, zh] = rows
-                    zo[a, 1 - zh] = jnp.zeros((HALF, BLK), F32)
-
-                @pl.when(z != to)
-                def _():
-                    send(zs.at[a, to], zr.at[a, step - 1], rz_s.at[a], rz_r.at[a, step - 1], {"zh": h, "zl": zp})
+
+                def keep():
+                    zo[a, h] = rows
+                    zo[a, 1 - h] = jnp.zeros((HALF, BLK), F32)
+
+                def pass_on():
+                    zs[a, 2 * p + h] = rows.astype(BF)
+                    step = rem(z + 8 - to, 8)
+                    send(zs.at[a, 2 * p + h], zr.at[a, step - 1], rz_s.at[0], rz_r.at[a], {"zh": h, "zl": zp})
+
+                if TURN[p] == 0:
+                    pl.when(zh == h)(keep)
+                    pl.when(zh != h)(pass_on)
+                else:
+                    pass_on()
 
     def finish(a):
-        for j in range(1, 8):
-            step = NEAR[j]
-            h = rem(z + step, 8) // 4
-            wait(zr.at[a, step - 1], rz_r.at[a, step - 1])
-            zo[a, h] += zr[a, step - 1].astype(F32)
+        wait(zr.at[a], rz_r.at[a])
+        for step in range(1, 8):
+            zo[a, rem(z + step, 8) // 4] += zr[a, step - 1].astype(F32)
         for h in range(2):
             fin[a, h] = zo[a, h].astype(BF)
             ret[a, cap(h * 4 + y), :] = fin[a, h, cap(y), :]
         for dy in range(1, 4):
             ty = rem(y + dy, 4)
             for h in range(2):
-                send(fin.at[a, h, cap(ty), :], ret.at[a, cap(h * 4 + y), :], b_s.at[a], b_r.at[a], {"y": ty})
+                send(fin.at[a, h, cap(ty), :], ret.at[a, cap(h * 4 + y), :], b_s.at[0], b_r.at[a], {"y": ty})
 
     def send_dots():
         @pl.loop(0, 8)
@@ -463,17 +474,35 @@
             wu[at, :] = (dot_tn(t0, PU[0, :, mine]) + dot_tn(t1, PU[1, :, mine])).astype(BF)
             wd[:, at] = (dot_tn(HS[0], G[1, :, at]) + dot_tn(HS[1], G[3, :, at])).astype(BF)
 
+    def send_router():
+        total = ar_end(1)
+        share = jnp.zeros((BLK, BLK), F32)
+        deltas = []
+        for m in range(2):
+            _, _, h0, h1 = hits(m)
+            delta = to_col(total[m : m + 1, :], BLK) * gates[m, 0] * gates[m, 1]
+            deltas.append(delta)
+            share = share + lax.dot_general(
+                delta * (h0 - h1), tok[m].astype(F32), (((0,), (0,)), ((), ())),
+                preferred_element_type=F32, precision=lax.Precision.HIGHEST,
+            )
+        rgs[...] = share[0:8, :]
+        for n, (dz, dy) in enumerate(PEERS):
+            tz, ty = rem(zh + dz, 2), rem(y + dy, 4)
+            send(rgs, rgr.at[n], rg_s.at[0], rg_r.at[0], {"zh": tz, "y": ty})
+        return deltas
+
     stage_a(0)
     stage_a(1)
     b_start()
     stage_a(2)
     ar_two(0)
+    stage_b(0)
     b_forward()
     ar_three(0)
+    stage_c(0)
     make_gates()
     b_spread()
-    stage_b(0)
-    stage_c(0)
     stage_b(1)
     stage_d(0)
     stage_c(1)
@@ -485,11 +514,12 @@
         wait(half, w_l.at[3 + k])
         wait(half, w_r.at[k])
     pre(0)
+    hid(0)
     stage_d(1)
-    stage_c(2)
     stage_e(1)
     take_gates()
     back(0)
+    stage_c(2)
     outs(0)
     far_sends(0)
     near_sends(0)
@@ -501,52 +531,45 @@
     b_take(0)
     stage_e(2)
     pre(1)
+    hid(1)
     b_take(1)
+    outs(1)
     second_sends(1)
+    far_sends(2)
+    near_sends(2)
     b_take(2)
     b_take(3)
+    third_sends(0)
     stage_e(3)
     back(1)
-    outs(1)
-    far_sends(2)
-    near_sends(2)
     send_dots()
     ins(1)
+    third_sends(1)
+    second_sends(2)
     far_sends(3)
-    second_sends(2)
-    near_sends(3)
-    third_sends(0)
-    third_sends(1)
+    near_sends(3, (0,))
+    take_dots()
     weight_grads(0, 3)
-    take_dots()
-    third_sends(2, (0, 1))
-    second_sends(3)
-    third_sends(2, (2, 3))
+    finish(0)
+    third_sends(2)
+    second_sends(3, (0,))
+    near_sends(3, (1,))
+    second_sends(3, (1,))
+    near_sends(3, (2,))
+    ar_two(1)
+    second_sends(3, (2,))
+    near_sends(3, (3,))
+    second_sends(3, (3,))
     weight_grads(3, 5)
-    finish(0)
-    ar_two(1)
     finish(1)
-    third_sends(3, (0, 1))
-    weight_grads(5, 7)
+    third_sends(3, (0,))
+    third_sends(3, (1,))
+    third_sends(3, (2,))
     ar_three(1)
-    third_sends(3, (2, 3))
-    weight_grads(7, 8)
-
-    total = ar_end(1)
-    share = jnp.zeros((BLK, BLK), F32)
-    deltas = []
-    for m in range(2):
-        _, _, h0, h1 = hits(m)
-        delta = to_col(total[m : m + 1, :], BLK) * gates[m, 0] * gates[m, 1]
-        deltas.append(delta)
-        share = share + lax.dot_general(
-            delta * (h0 - h1), tok[m].astype(F32), (((0,), (0,)), ((), ())),
-            preferred_element_type=F32, precision=lax.Precision.HIGHEST,
-        )
-    rgs[...] = share[0:8, :]
-    for n, (dz, dy) in enumerate(PEERS):
-        tz, ty = rem(zh + dz, 2), rem(y + dy, 4)
-        send(rgs, rgr.at[n], rg_s.at[0], rg_r.at[n], {"zh": tz, "y": ty})
+    third_sends(3, (3,))
+    weight_grads(5, 6)
+    deltas = send_router()
+    weight_grads(6, 8)
     finish(2)
     finish(3)
 
@@ -569,31 +592,24 @@
         tgrad[m] = grad.astype(BF)
 
     whole = rgs[...]
+    wait(rgr.at[0:7], rg_r.at[0])
     for n in range(7):
-        wait(rgr.at[n], rg_r.at[n])
         whole = whole + rgr[n]
     rg[...] = whole
 
-    for arr in range(4):
-        wait(snd.at[arr, 0:288, :], a_s.at[arr])
-        if arr < 3:
-            wait(G.at[arr, 0:HALF, 0:896], z_s.at[arr])
-            wait(G.at[arr, :, 0:1536], x_s.at[arr])
-        wait(G.at[arr, :, 0:2048], d_s.at[arr])
-        wait(Pt.at[arr, :, 0:1536], rx_s.at[arr])
-        wait(zr.at[arr], rz_s.at[arr])
-        wait(ret.at[arr, 0:288, :], b_s.at[arr])
+    wait(snd.at[:, 0:288, :], a_s.at[0])
+    wait(G.at[0:3, 0:HALF, 0:896], z_s.at[0])
+    wait(G.at[0:3, :, 0:1536], x_s.at[0])
+    wait(G.at[:, :, 0:2048], d_s.at[0])
+    wait(Pt.at[:, :, 0:1536], rx_s.at[0])
+    wait(zr, rz_s.at[0])
+    wait(ret.at[:, 0:288, :], b_s.at[0])
     wait(zr.at[0, 0:6], xb_s.at[0])
     wait(G.at[3, 0:HALF, 0:3584], z3_s.at[0])
     for k, half in enumerate((WgH.at[:, 0:HID], WuH.at[:, 0:HID], WdH.at[0:HID, :])):
         wait(half, w_s.at[k])
-    for m in range(2):
-        for n, buf in enumerate((HC, PG, PU)):
-            wait(buf.at[m, :, 0:HID], h_s.at[m, n])
-    for k in range(2):
-        wait(arR.at[k, 0:3], ar_s.at[k, 0])
-        wait(arR.at[k, 3:6], ar_s.at[k, 1])
-        wait(arR.at[k, 6], ar_s.at[k, 2])
+    wait(G.at[0, :, 0:1536], h_s.at[0])
+    wait(arR, ar_s.at[0])
     wait(gts.at[0:7], gt_s.at[0])
     wait(dts.at[0:7], dt_s.at[0])
     wait(rgr.at[0:7], rg_s.at[0])
@@ -634,10 +650,10 @@
             wide(2, 2, BLK, BLK), wide(2, 2, BLK, BLK), wide(2, BLK, BLK),
             wide(2, 3, 8, BLK), wide(2, 7, 8, BLK), wide(8, 8, BLK), wide(8, 8, BLK), wide(8, 8, BLK), wide(8, 8, BLK),
             wide(8, BLK), wide(7, 8, BLK),
-            dma(6), dma(3), dma(3), dma(4), dma(4), dma(4), dma(3, 8), dma(4), dma(3, 8), dma(3, 8), dma(3, 8),
-            dma(4), dma(4), dma(2, 3), dma(2, 3),
-            dma(4), dma(4, 4), dma(4, 4), dma(4, 4), dma(4), dma(4, 7), dma(4), dma(4),
-            dma(2, 3), dma(2, 7), dma(1), dma(1), dma(1), dma(1), dma(1), dma(7), dma(1), dma(4), dma(1), dma(4, 8),
+            dma(6), dma(3), dma(3), dma(1), dma(4), dma(1), dma(3, 8), dma(1), dma(3, 8), dma(3, 8), dma(3, 8),
+            dma(1), dma(4), dma(1), dma(2, 3),
+            dma(1), dma(4, 4), dma(4, 4), dma(4, 4), dma(1), dma(4), dma(1), dma(4),
+            dma(1), dma(2, 3), dma(1), dma(1), dma(1), dma(1), dma(1), dma(1), dma(1), dma(4), dma(1), dma(4),
         ],
         compiler_params=pltpu.CompilerParams(
             collective_id=0, has_side_effects=True, vmem_limit_bytes=52 * 1024 * 1024

time: 143 us -> 127 us (0.89)
  Pallas kernels: 140 us -> 126 us
    pallas_call x1, Pallas kernels: 138 us -> 123 us  [shards(): pl.pallas_call(kernel, name='expert_layer', out_shape=(big(2, BLK, BLK),...]
where the time goes in v3:
time: 127 us; the launch traced here: 126 us
  Pallas kernels  126 us (99%)
    pallas_call x1, Pallas kernels, shards(): pl.pallas_call(kernel, name='expert_layer', out_shape=(big(2, BLK, BLK),...  123 us
    pallas_call x1, Pallas kernels, shards(): pl.pallas_call(write_out, name='write_out', out_shape=tuple((jax.ShapeDty...  2.8 us

profile of v3, /device:TPU:32, one launch (start us, length us, event | category | flops | bytes accessed | tf_op | source)
XLA Modules:
  0.0 126.4 jit_solution(10733393601680720673)
XLA Ops:
  0.6 122.8 %expert_layer.1 = (bf16[2,128,128]{2,1,0:T(8,128)(2,1)S(1)}, bf16[2,128,128]{2,1,0:T(8,128)(2,1)S(1)}, bf16[4096,256]{1,0:T(8,128)(2,1)S(1)}, bf16[4096,256]{1,0...) custom-call(bf16[2,128,128]{2,1,0:T(8,128)(2,1)} %tok.1, bf16[2,128,128]{2,1,0:T(8,128)(2,1)} %cot.1, ...), custom_call_target="tpu_custom_call" | custom-call | tf_op jit(solution)/shard_map/expert_layer/pallas_call | solution.py:634
  123.5 2.8 %write_out.1 = (bf16[2,128,128]{2,1,0:T(8,128)(2,1)}, bf16[2,128,128]{2,1,0:T(8,128)(2,1)}, bf16[4096,256]{1,0:T(8,128)(2,1)}, bf16[4096,256]{1,0:T(8,128)(2,1)}...) custom-call(bf16[2,128,128]{2,1,0:T(8,128)(2,1)S(1)} %get-tuple-element.18.refs_0_, ...), custom_call_target="tpu_custom_call" | custom-call | tf_op jit(solution)/shard_map/write_out/pallas_call | solution.py:662

commit v4 on v3

--- a/solution.py
+++ b/solution.py
@@ -66,10 +66,10 @@
 def kernel(
     tok, cot, ids, rwt, wg_h, wu_h, wd_h,
     mixed, tgrad, wg, wu, wd, rg,
-    G, WgH, WuH, WdH, snd, HB, XB, AG, AU, HG, HC, PG, PU, HS, gcol, dcol,
+    G, WgH, WuH, WdH, snd, HB, XB, HX, AG, AU, HG, HC, PG, PU, HS, gcol, dcol,
     Pt, FX, XL, XR, zs, zr, zo, fin, ret, slots, gates, dmat, arS, arR, gts, gtr, dts, dtr, rgs, rgr,
     w_l, w_s, w_r, a_s, a_r, z_s, z_r, x_s, xl_r, xr_r, f_r, d_s, d_r, h_s, h_r,
-    rx_s, rf_r, rl_r, rr_r, rz_s, rz_r, b_s, b_r, ar_s, ar_r, gt_s, gt_r, dt_s, dt_r, rg_s, rg_r, xb_s, xb_r, z3_s, z3_r,
+    rx_s, rf_r, rl_r, rr_r, rz_s, rz_r, b_s, b_r, ar_s, ar_r, gt_s, gt_r, dt_s, dt_r, rg_s, rg_r, xb_s, xb_r, z3_s, z3_r, by_s, by_r,
 ):
     zl = lax.axis_index("zl")
     x = lax.axis_index("x")
@@ -144,8 +144,8 @@
         dmat[m] = diff
         return to_row(jnp.sum(tok[m].astype(F32) * diff, axis=1, keepdims=True))
 
-    def y_sends(m):
-        for arr in (2 * m, 2 * m + 1):
+    def y_sends(*arrs):
+        for arr in arrs:
             for dy in range(1, 4):
                 ty = rem(y + dy, 4)
                 for h in range(2):
@@ -181,11 +181,13 @@
         return arS[k, 2] + arR[k, 6]
 
 
-    y_sends(0)
+    y_sends(0, 1)
     arS[0, 0] = tile_of([logits(0), logits(1)])
     ar_one(0)
     route(1)
-    y_sends(1)
+    send(snd.at[3], XB.at[0], xb_s.at[0], xb_r.at[0], {"x": right})
+    send(snd.at[3], XB.at[1], xb_s.at[0], xb_r.at[1], {"x": left})
+    y_sends(2)
 
     pltpu.make_async_copy(wg_h, wg, w_l.at[0]).start()
     pltpu.make_async_copy(wu_h, wu, w_l.at[1]).start()
@@ -246,16 +248,28 @@
                 send(here, here, x_s.at[0], f_r.at[arr, j], {"x": left})
             send(here, here, d_s.at[0], d_r.at[arr], {"c": oc})
 
-    def b_start():
-        wait(snd.at[3, 0:288, :], a_r.at[3])
-        send(HB.at[3], XB.at[0], xb_s.at[0], xb_r.at[0], {"x": right})
-        send(HB.at[3], XB.at[1], xb_s.at[0], xb_r.at[1], {"x": left})
-
     def b_forward():
         wait(XB.at[0], xb_r.at[0])
-        send(XB.at[0, 0], XB.at[2, 0], xb_s.at[0], xb_r.at[2], {"x": right})
+        send(XB.at[0, 0:HALF, :], XB.at[2, 0:HALF, :], xb_s.at[0], xb_r.at[2], {"x": right})
         wait(XB.at[1], xb_r.at[1])
-        send(XB.at[1, 1], XB.at[2, 1], xb_s.at[0], xb_r.at[3], {"x": left})
+        send(XB.at[1, HALF:, :], XB.at[2, HALF:, :], xb_s.at[0], xb_r.at[3], {"x": left})
+
+    def b_y(q):
+        src = snd.at[3] if q == 0 else XB.at[q - 1]
+        for h in range(2):
+            if q > 0:
+                HX[q, h, cap(y), :] = src[cap(h * 4 + y), :]
+            else:
+                HX[q, h, cap(y), :] = HB[3, h, cap(y), :]
+        for dy in range(1, 4):
+            ty = rem(y + dy, 4)
+            for h in range(2):
+                send(src.at[cap(h * 4 + ty), :], HX.at[q, h, cap(y), :], by_s.at[0], by_r.at[q], {"y": ty})
+
+    def b_far():
+        wait(XB.at[2, 0:HALF, :], xb_r.at[2])
+        wait(XB.at[2, HALF:, :], xb_r.at[3])
+        b_y(3)
 
     def b_out(q, src, x_):
         here = place(3, z, x_)
@@ -266,12 +280,9 @@
         send(here, here, d_s.at[0], d_r.at[3], {"c": oc})
 
     def b_spread():
-        b_out(0, HB.at[3], x)
-        b_out(1, XB.at[0], left)
-        b_out(2, XB.at[1], right)
-        wait(XB.at[2, 0], xb_r.at[2])
-        wait(XB.at[2, 1], xb_r.at[3])
-        b_out(3, XB.at[2], far)
+        for q, x_ in enumerate((x, left, right, far)):
+            wait(snd.at[3, 0:288, :], by_r.at[q])
+            b_out(q, HX.at[q], x_)
 
     def b_take(q):
         wait(zr.at[0], z3_r.at[q])
@@ -494,11 +505,14 @@
 
     stage_a(0)
     stage_a(1)
-    b_start()
     stage_a(2)
     ar_two(0)
+    b_y(0)
+    b_forward()
+    b_y(1)
+    b_y(2)
     stage_b(0)
-    b_forward()
+    b_far()
     ar_three(0)
     stage_c(0)
     make_gates()
@@ -597,7 +611,8 @@
         whole = whole + rgr[n]
     rg[...] = whole
 
-    wait(snd.at[:, 0:288, :], a_s.at[0])
+    wait(snd.at[0:3, 0:288, :], a_s.at[0])
+    wait(snd.at[:, 0:288, :], by_s.at[0])
     wait(G.at[0:3, 0:HALF, 0:896], z_s.at[0])
     wait(G.at[0:3, :, 0:1536], x_s.at[0])
     wait(G.at[:, :, 0:2048], d_s.at[0])
@@ -641,7 +656,7 @@
         out_specs=(vm,) * 6,
         scratch_shapes=[
             big(4, ROWS, D),
-            big(2048, 512), big(2048, 512), big(512, 2048), big(4, ROWS, BLK), big(4, 2, HALF, BLK), big(3, 2, HALF, BLK),
+            big(2048, 512), big(2048, 512), big(512, 2048), big(4, ROWS, BLK), big(4, 2, HALF, BLK), big(3, ROWS, BLK), big(4, 2, HALF, BLK),
             wide(ROWS, HID), wide(ROWS, HID), wide(ROWS, HID),
             big(2, ROWS, 512), big(2, ROWS, 512), big(2, ROWS, 512), big(2, ROWS, HID),
             wide(2, ROWS, BLK), wide(2, ROWS, BLK),
@@ -650,10 +665,10 @@
             wide(2, 2, BLK, BLK), wide(2, 2, BLK, BLK), wide(2, BLK, BLK),
             wide(2, 3, 8, BLK), wide(2, 7, 8, BLK), wide(8, 8, BLK), wide(8, 8, BLK), wide(8, 8, BLK), wide(8, 8, BLK),
             wide(8, BLK), wide(7, 8, BLK),
-            dma(6), dma(3), dma(3), dma(1), dma(4), dma(1), dma(3, 8), dma(1), dma(3, 8), dma(3, 8), dma(3, 8),
+            dma(6), dma(3), dma(3), dma(1), dma(3), dma(1), dma(3, 8), dma(1), dma(3, 8), dma(3, 8), dma(3, 8),
             dma(1), dma(4), dma(1), dma(2, 3),
             dma(1), dma(4, 4), dma(4, 4), dma(4, 4), dma(1), dma(4), dma(1), dma(4),
-            dma(1), dma(2, 3), dma(1), dma(1), dma(1), dma(1), dma(1), dma(1), dma(1), dma(4), dma(1), dma(4),
+            dma(1), dma(2, 3), dma(1), dma(1), dma(1), dma(1), dma(1), dma(1), dma(1), dma(4), dma(1), dma(4), dma(1), dma(4),
         ],
         compiler_params=pltpu.CompilerParams(
             collective_id=0, has_side_effects=True, vmem_limit_bytes=52 * 1024 * 1024

time: 127 us -> 126 us (level)
  no operation moved by 1% of the time
where the time goes in v4:
time: 126 us
  Pallas kernels  125 us (99%)
    pallas_call x1, Pallas kernels, shards(): pl.pallas_call(kernel, name='expert_layer', out_shape=(big(2, BLK, BLK),...  122 us
    pallas_call x1, Pallas kernels, shards(): pl.pallas_call(write_out, name='write_out', out_shape=tuple((jax.ShapeDty...  2.8 us

profile of v4, /device:TPU:32, one launch (start us, length us, event | category | flops | bytes accessed | tf_op | source)
XLA Modules:
  0.0 126.0 jit_solution(10841213060803709504)
XLA Ops:
  0.6 122.4 %expert_layer.1 = (bf16[2,128,128]{2,1,0:T(8,128)(2,1)S(1)}, bf16[2,128,128]{2,1,0:T(8,128)(2,1)S(1)}, bf16[4096,256]{1,0:T(8,128)(2,1)S(1)}, bf16[4096,256]{1,0...) custom-call(bf16[2,128,128]{2,1,0:T(8,128)(2,1)} %tok.1, bf16[2,128,128]{2,1,0:T(8,128)(2,1)} %cot.1, ...), custom_call_target="tpu_custom_call" | custom-call | tf_op jit(solution)/shard_map/expert_layer/pallas_call | solution.py:649
  123.0 2.8 %write_out.1 = (bf16[2,128,128]{2,1,0:T(8,128)(2,1)}, bf16[2,128,128]{2,1,0:T(8,128)(2,1)}, bf16[4096,256]{1,0:T(8,128)(2,1)}, bf16[4096,256]{1,0:T(8,128)(2,1)}...) custom-call(bf16[2,128,128]{2,1,0:T(8,128)(2,1)S(1)} %get-tuple-element.18.refs_0_, ...), custom_call_target="tpu_custom_call" | custom-call | tf_op jit(solution)/shard_map/write_out/pallas_call | solution.py:677

commit v5 on v4

--- a/solution.py
+++ b/solution.py
@@ -240,12 +240,12 @@
             here = place(arr, zj, left)
             wait(here, xl_r.at[arr, j])
             if j % 2 == 0:
-                send(here, here, x_s.at[0], f_r.at[arr, j], {"x": right})
+                send(here, here, x_s.at[0], f_r.at[arr], {"x": right})
             send(here, here, d_s.at[0], d_r.at[arr], {"c": oc})
             here = place(arr, zj, right)
             wait(here, xr_r.at[arr, j])
             if j % 2 == 1:
-                send(here, here, x_s.at[0], f_r.at[arr, j], {"x": left})
+                send(here, here, x_s.at[0], f_r.at[arr], {"x": left})
             send(here, here, d_s.at[0], d_r.at[arr], {"c": oc})
 
     def b_forward():
@@ -291,9 +291,9 @@
             send(here, here, d_s.at[0], d_r.at[3], {"c": oc})
 
     def stage_d(arr):
+        wait(fin, f_r.at[arr])
         for j in range(8):
             here = place(arr, rem(z + NEAR[j], 8), far)
-            wait(here, f_r.at[arr, j])
             send(here, here, d_s.at[0], d_r.at[arr], {"c": oc})
 
     def stage_e(arr):
@@ -590,7 +590,6 @@
     for m in range(2):
         a = 2 * m
         wait(ret.at[a, 0:288, :], b_r.at[a])
-        wait(ret.at[a + 1, 0:288, :], b_r.at[a + 1])
         one = jnp.zeros((BLK, BLK), F32)
         two = jnp.zeros((BLK, BLK), F32)
         grad = deltas[m] * dmat[m]
@@ -601,8 +600,12 @@
             rows = ret[a, q * BLK : (q + 1) * BLK, :]
             one = one + dot(p0.astype(BF), rows)
             two = two + dot(p1.astype(BF), rows)
-            grad = grad + dot((p0 + p1).astype(BF), ret[a + 1, q * BLK : (q + 1) * BLK, :])
         mixed[m] = (gates[m, 0] * one + gates[m, 1] * two).astype(BF)
+        wait(ret.at[a + 1, 0:288, :], b_r.at[a + 1])
+        for q in range(3):
+            at = lane + float(q * BLK)
+            both = jnp.where((slots[m, 0] == at) | (slots[m, 1] == at), 1.0, 0.0)
+            grad = grad + dot(both.astype(BF), ret[a + 1, q * BLK : (q + 1) * BLK, :])
         tgrad[m] = grad.astype(BF)
 
     whole = rgs[...]
@@ -665,7 +668,7 @@
             wide(2, 2, BLK, BLK), wide(2, 2, BLK, BLK), wide(2, BLK, BLK),
             wide(2, 3, 8, BLK), wide(2, 7, 8, BLK), wide(8, 8, BLK), wide(8, 8, BLK), wide(8, 8, BLK), wide(8, 8, BLK),
             wide(8, BLK), wide(7, 8, BLK),
-            dma(6), dma(3), dma(3), dma(1), dma(3), dma(1), dma(3, 8), dma(1), dma(3, 8), dma(3, 8), dma(3, 8),
+            dma(6), dma(3), dma(3), dma(1), dma(3), dma(1), dma(3, 8), dma(1), dma(3, 8), dma(3, 8), dma(3),
             dma(1), dma(4), dma(1), dma(2, 3),
             dma(1), dma(4, 4), dma(4, 4), dma(4, 4), dma(1), dma(4), dma(1), dma(4),
             dma(1), dma(2, 3), dma(1), dma(1), dma(1), dma(1), dma(1), dma(1), dma(1), dma(4), dma(1), dma(4), dma(1), dma(4),

time: 126 us -> 126 us (level)
  no operation moved by 1% of the time
where the time goes in v5:
time: 126 us; the launch traced here: 125 us
  Pallas kernels  124 us (98%)
    pallas_call x1, Pallas kernels, shards(): pl.pallas_call(kernel, name='expert_layer', out_shape=(big(2, BLK, BLK),...  121 us
    pallas_call x1, Pallas kernels, shards(): pl.pallas_call(write_out, name='write_out', out_shape=tuple((jax.ShapeDty...  2.8 us

profile of v5, /device:TPU:32, one launch (start us, length us, event | category | flops | bytes accessed | tf_op | source)
XLA Modules:
  0.0 124.9 jit_solution(9051101807993967924)
XLA Ops:
  0.6 121.3 %expert_layer.1 = (bf16[2,128,128]{2,1,0:T(8,128)(2,1)S(1)}, bf16[2,128,128]{2,1,0:T(8,128)(2,1)S(1)}, bf16[4096,256]{1,0:T(8,128)(2,1)S(1)}, bf16[4096,256]{1,0...) custom-call(bf16[2,128,128]{2,1,0:T(8,128)(2,1)} %tok.1, bf16[2,128,128]{2,1,0:T(8,128)(2,1)} %cot.1, ...), custom_call_target="tpu_custom_call" | custom-call | tf_op jit(solution)/shard_map/expert_layer/pallas_call | solution.py:652
  122.0 2.8 %write_out.1 = (bf16[2,128,128]{2,1,0:T(8,128)(2,1)}, bf16[2,128,128]{2,1,0:T(8,128)(2,1)}, bf16[4096,256]{1,0:T(8,128)(2,1)}, bf16[4096,256]{1,0:T(8,128)(2,1)}...) custom-call(bf16[2,128,128]{2,1,0:T(8,128)(2,1)S(1)} %get-tuple-element.18.refs_0_, ...), custom_call_target="tpu_custom_call" | custom-call | tf_op jit(solution)/shard_map/write_out/pallas_call | solution.py:680
